TPU v7x, 128 devices: a whole 4x4x4 slice. The times are simulated.
128 devices in a mesh: row: 8 (over z, core), col: 16 (over y, x).
Axes of the slice: x: 4, y: 4, z: 4, core: 2. Of those that a mesh axis runs over, the one named last changes fastest.
Arguments:
- right_side: float32 [512, 4096], P('row', 'col'), may hold values from -20 to 20
- initial_guess: float32 [512, 4096], P('row', 'col'), may hold values from -3 to 3
- kernel: float32 [31, 31], replicated, may hold values from 0 to 1, as said below
Outputs:
- template: float32 [512, 4096], P('row', 'col')
- residual: float32 [512, 4096], P('row', 'col')
Inputs may be any that keep to these rules, and one draw needn't show every extreme that they name: `kernel`: entries are positive and sum to one.
All inputs are finite; a program needn't handle non-finite values.
Results may differ from a plain program's by a relative error of at most 0.0003.
Values sent between devices are 32-bit elements; how exact they have to be, the bound alone decides.
A program may use at most 128 MiB of HBM per device.

v0:
```python
import math

import jax
import jax.numpy as jnp
from jax import lax
from jax.sharding import Mesh
from jax.sharding import PartitionSpec as P

ITERS = 3
ROW_COL = ("row_0", "row_1", "col_0", "col_1")
ROW = ("row_0", "row_1")
COL = ("col_0", "col_1")


penalty = 0.05


def with_halo(x, sides, width):
    for axis, dim in sides:
        count, length = (lax.axis_size(axis), x.shape[dim])
        up = [(i, (i + 1) % count) for i in range(count - 1)]
        down = [(j, i) for i, j in up]
        last = lax.slice_in_dim(x, length - width, length, axis=dim)
        initial = lax.slice_in_dim(x, 0, width, axis=dim)
        before = lax.ppermute(last, axis, up)
        after = lax.ppermute(initial, axis, down)
        x = jnp.concatenate([before, x, after], axis=dim)
    return x


def one_axis_at_a_time(x, axes):
    for axis in axes:
        x = lax.psum(x, axis)
    return x


def banded_tables(taps, block_width):
    width = taps.shape[0]
    span = block_width + width - 1
    offset = (
        jnp.arange(span, dtype=jnp.int32)[:, None]
        - jnp.arange(block_width, dtype=jnp.int32)[None, :]
    )
    selector = (offset[None, :, :] == jnp.arange(width, dtype=jnp.int32)[:, None, None]).astype(
        jnp.float32
    )
    return jnp.einsum("ab,bkj->akj", taps, selector, precision=lax.Precision.HIGHEST)


def correlate(padded, taps):
    width = taps.shape[0]
    out_rows = padded.shape[0] - width + 1
    out_cols = padded.shape[1] - width + 1
    block_width = math.gcd(out_cols, 128)
    count = out_cols // block_width
    span = block_width + width - 1
    tables = banded_tables(taps, block_width)
    blocks = jnp.stack(
        [padded[:, index * block_width : index * block_width + span] for index in range(count)],
        axis=1,
    )
    total = jnp.zeros((out_rows, count, block_width), jnp.float32)
    for shift_row in range(width):
        window = blocks[shift_row : shift_row + out_rows]
        total = total + jnp.einsum(
            "rnk,kj->rnj", window, tables[shift_row], precision=lax.Precision.HIGHEST
        )
    return total.reshape(out_rows, out_cols)


def laplacian(padded, margin, tile_rows, tile_cols):
    center = padded[margin : margin + tile_rows, margin : margin + tile_cols]
    upper = padded[margin - 1 : margin - 1 + tile_rows, margin : margin + tile_cols]
    lower = padded[margin + 1 : margin + 1 + tile_rows, margin : margin + tile_cols]
    leftward = padded[margin : margin + tile_rows, margin - 1 : margin - 1 + tile_cols]
    rightward = padded[margin : margin + tile_rows, margin + 1 : margin + 1 + tile_cols]
    return 4.0 * center - upper - lower - leftward - rightward


def operate(source, kernel):
    tile_rows, tile_cols = source.shape
    half_width = kernel.shape[0] // 2
    flipped = kernel[::-1, ::-1]
    padded = with_halo(source, ((ROW, 0), (COL, 1)), half_width)
    blurred = correlate(padded, kernel)
    blurred_pad = with_halo(blurred, ((ROW, 0), (COL, 1)), half_width)
    back = correlate(blurred_pad, flipped)
    smooth_term = laplacian(padded, half_width, tile_rows, tile_cols)
    return back + penalty * smooth_term


def paired(residual, applied):
    return (
        one_axis_at_a_time(jnp.sum(residual * residual), ROW_COL),
        one_axis_at_a_time(jnp.sum(residual * applied), ROW_COL),
    )


def on_device(right_side, initial_guess, kernel):
    template = initial_guess
    residual = right_side - operate(template, kernel)
    applied = operate(residual, kernel)
    norm_now, product = paired(residual, applied)
    step_size = norm_now / product
    direction, along = (residual, applied)
    for iteration in range(ITERS):
        template = template + step_size * direction
        residual = residual - step_size * along
        if iteration + 1 < ITERS:
            applied = operate(residual, kernel)
            norm_next, product = paired(residual, applied)
            ratio = norm_next / norm_now
            step_size = norm_next / (product - ratio * norm_next / step_size)
            direction = residual + ratio * direction
            along = applied + ratio * along
            norm_now = norm_next
    return (template, residual)


def solution(mesh):
    torus = Mesh(mesh.devices.reshape(4, 2, 4, 4), ("row_0", "row_1", "col_0", "col_1"))
    placed = (P(ROW, COL), P(ROW, COL), P())
    return jax.shard_map(
        on_device,
        mesh=torus,
        in_specs=placed,
        out_specs=(P(ROW, COL), P(ROW, COL)),
        check_vma=False,
    )
```

profile of v0, /device:TPU:2, one launch (start us, length us, event | category | flops | bytes accessed | tf_op | source)
XLA Modules:
  0.0 353.4 jit_solution(8451478255131608723)
XLA Ops:
  1.4 1.7 collective-permute-start
  3.1 1.3 collective-permute-start.1
  5.2 2.0 fusion.2
  7.3 1.3 fusion.3
  8.6 1.3 fusion.1273
  10.0 1.3 fusion.1275
  11.4 1.9 collective-permute-start.3
  13.4 4.5 %collective-permute-start.2 = (f32[94,15]{1,0:T(8,128)S(1)}, f32[94,15]{1,0:T(8,128)S(1)}, u32[]{:S(2)}, u32[]{:S(2)}) collective-permute-start(f32[94,15]{1,0:T(8,128)S(1)} %get-tuple-element.128), channel_id=1, source_target_pairs={{0,1},{1,2},{2,3},{3,4},{4,5},{5,6},{6,7},{7,8},{8,9},{9,10},{10,1... | collective-permute-start | bytes 16928 | tf_op jit(solution)/shard_map/ppermute | solution.py:25
  28.0 1.3 collective-permute-start.5
  29.3 4.4 %collective-permute-start.4 = (f32[15,256]{1,0:T(8,128)S(1)}, f32[15,256]{1,0:T(8,128)S(1)}, u32[]{:S(2)}, u32[]{:S(2)}) collective-permute-start(f32[15,256]{1,0:T(8,128)S(1)} %bitcast.674), channel_id=1, source_target_pairs={{0,16},{16,32},{32,48},{48,64},{64,80},{80,96},{96,112},{1,17},{17... | collective-permute-start | bytes 46088 | tf_op jit(solution)/shard_map/ppermute | solution.py:25
  34.7 2.2 collective-permute-start.7
  36.9 3.8 %collective-permute-start.6 = (f32[94,15]{1,0:T(8,128)S(1)}, f32[94,15]{1,0:T(8,128)S(1)}, u32[]{:S(2)}, u32[]{:S(2)}) collective-permute-start(f32[94,15]{1,0:T(8,128)S(1)} %get-tuple-element.124), channel_id=1, source_target_pairs={{0,1},{1,2},{2,3},{3,4},{4,5},{5,6},{6,7},{7,8},{8,9},{9,10},{10,1... | collective-permute-start | bytes 16928 | tf_op jit(solution)/shard_map/ppermute | solution.py:25
  41.6 1.3 collective-permute-done.6
  51.5 3.7 %collective-permute-start.8 = (f32[15,256]{1,0:T(8,128)S(1)}, f32[15,256]{1,0:T(8,128)S(1)}, u32[]{:S(2)}, u32[]{:S(2)}) collective-permute-start(f32[15,256]{1,0:T(8,128)S(1)} %get-tuple-element.141), channel_id=1, source_target_pairs={{0,16},{16,32},{32,48},{48,64},{64,80},{80,96},{96,112},{1,17},{17... | collective-permute-start | bytes 46088 | tf_op jit(solution)/shard_map/ppermute | solution.py:25
  55.2 1.3 collective-permute-start.9
  56.5 4.7 %collective-permute-done.9 = f32[15,256]{1,0:T(8,128)S(1)} collective-permute-done((f32[15,256]{1,0:T(8,128)S(1)}, f32[15,256]{1,0:T(8,128)S(1)}, u32[]{:S(2)}, u32[]{:S(2)}) %collective-permute-start.9) | collective-permute-done | bytes 15392 | tf_op jit(solution)/shard_map/ppermute | solution.py:26
  61.3 3.9 %collective-permute-start.10 = (f32[94,15]{1,0:T(8,128)S(1)}, f32[94,15]{1,0:T(8,128)S(1)}, u32[]{:S(2)}, u32[]{:S(2)}) collective-permute-start(f32[94,15]{1,0:T(8,128)S(1)} %get-tuple-element.119), channel_id=1, source_target_pairs={{0,1},{1,2},{2,3},{3,4},{4,5},{5,6},{6,7},{7,8},{8,9},{9,10},{10,1... | collective-permute-start | bytes 16928 | tf_op jit(solution)/shard_map/ppermute | solution.py:25
  65.3 2.1 collective-permute-start.11
  67.4 5.9 %collective-permute-done.11 = f32[94,15]{1,0:T(8,128)S(1)} collective-permute-done((f32[94,15]{1,0:T(8,128)S(1)}, f32[94,15]{1,0:T(8,128)S(1)}, u32[]{:S(2)}, u32[]{:S(2)}) %collective-permute-start.11) | collective-permute-done | bytes 5672 | tf_op jit(solution)/shard_map/ppermute | solution.py:26
  82.1 1.3 collective-permute-start.13
  83.4 3.8 %collective-permute-start.12 = (f32[15,256]{1,0:T(8,128)S(1)}, f32[15,256]{1,0:T(8,128)S(1)}, u32[]{:S(2)}, u32[]{:S(2)}) collective-permute-start(f32[15,256]{1,0:T(8,128)S(1)} %bitcast.675), channel_id=1, source_target_pairs={{0,16},{16,32},{32,48},{48,64},{64,80},{80,96},{96,112},{1,17},{17... | collective-permute-start | bytes 46088 | tf_op jit(solution)/shard_map/ppermute | solution.py:25
  88.1 1.9 collective-permute-start.15
  90.1 6.6 %collective-permute-start.14 = (f32[94,15]{1,0:T(8,128)S(1)}, f32[94,15]{1,0:T(8,128)S(1)}, u32[]{:S(2)}, u32[]{:S(2)}) collective-permute-start(f32[94,15]{1,0:T(8,128)S(1)} %get-tuple-element.116), channel_id=1, source_target_pairs={{0,1},{1,2},{2,3},{3,4},{4,5},{5,6},{6,7},{7,8},{8,9},{9,10},{10,1... | collective-permute-start | bytes 16928 | tf_op jit(solution)/shard_map/ppermute | solution.py:25
  96.7 1.5 collective-permute-done.14
  107.6 14.4 %all-reduce.8 = (f32[]{:T(128)}, f32[]{:T(128)}) all-reduce(f32[]{:T(128)} %get-tuple-element.7, f32[]{:T(128)} %get-tuple-element.6), channel_id=1, replica_groups=mesh['row_0'=4,'row_1'=2,'col_0'=4,'col_1'=4] {'row_0'}, use_global_device_ids=true, to_apply=%region_1.0 | all-reduce | flops 2 | bytes 16 | tf_op jit(solution)/shard_map/psum | solution.py:33
  122.0 3.1 all-reduce.11
  125.1 16.4 %all-reduce.5 = (f32[]{:T(128)}, f32[]{:T(128)}) all-reduce(f32[]{:T(128)} %get-tuple-element.30, f32[]{:T(128)} %get-tuple-element.31), channel_id=1, replica_groups=mesh['row_0'=4,'row_1'=2,'col_0'=4,'col_1'=4] {'col_0'}, use_global_device_ids=true, to_apply=%region_3.0 | all-reduce | flops 2 | bytes 16 | tf_op jit(solution)/shard_map/psum | solution.py:33
  141.4 12.5 %all-reduce.2 = (f32[]{:T(128)}, f32[]{:T(128)}) all-reduce(f32[]{:T(128)} %get-tuple-element.18, f32[]{:T(128)} %get-tuple-element.19), channel_id=1, replica_groups=mesh['row_0'=4,'row_1'=2,'col_0'=4,'col_1'=4] {'col_1'}, use_global_device_ids=true, to_apply=%region_4.0 | all-reduce | flops 2 | bytes 16 | tf_op jit(solution)/shard_map/psum | solution.py:33
  155.2 1.3 collective-permute-start.16
  156.5 1.3 collective-permute-start.17
  157.8 1.8 collective-permute-done.17
  159.7 1.9 collective-permute-start.18
  161.6 4.3 %collective-permute-start.19 = (f32[94,15]{1,0:T(8,128)S(1)}, f32[94,15]{1,0:T(8,128)S(1)}, u32[]{:S(2)}, u32[]{:S(2)}) collective-permute-start(f32[94,15]{1,0:T(8,128)S(1)} %get-tuple-element.112), channel_id=1, source_target_pairs={{1,0},{2,1},{3,2},{4,3},{5,4},{6,5},{7,6},{8,7},{9,8},{10,9},{11,1... | collective-permute-start | bytes 16928 | tf_op jit(solution)/shard_map/ppermute | solution.py:26
  166.0 1.8 collective-permute-done.19
  167.9 1.2 fusion.196
  171.4 1.2 convolution_add_fusion.117
  172.6 1.2 convolution_add_fusion.116
  176.0 1.2 convolution_add_fusion.113
  184.5 1.3 collective-permute-start.21
  185.8 3.2 collective-permute-start.20
  190.0 3.7 %collective-permute-start.23 = (f32[94,15]{1,0:T(8,128)S(1)}, f32[94,15]{1,0:T(8,128)S(1)}, u32[]{:S(2)}, u32[]{:S(2)}) collective-permute-start(f32[94,15]{1,0:T(8,128)S(1)} %get-tuple-element.107), channel_id=1, source_target_pairs={{1,0},{2,1},{3,2},{4,3},{5,4},{6,5},{7,6},{8,7},{9,8},{10,9},{11,1... | collective-permute-start | bytes 16928 | tf_op jit(solution)/shard_map/ppermute | solution.py:26
  193.7 2.6 collective-permute-start.22
  196.4 3.4 collective-permute-done.22
  208.4 1.4 multiply_reduce_fusion.2
  209.8 12.8 %all-reduce.7 = (f32[]{:T(128)}, f32[]{:T(128)}) all-reduce(f32[]{:T(128)} %get-tuple-element.5, f32[]{:T(128)} %get-tuple-element.4), channel_id=1, replica_groups=mesh['row_0'=4,'row_1'=2,'col_0'=4,'col_1'=4] {'row_0'}, use_global_device_ids=true, to_apply=%region_11.0 | all-reduce | flops 2 | bytes 16 | tf_op jit(solution)/shard_map/psum | solution.py:33
  222.5 3.1 all-reduce.10
  225.7 10.3 %all-reduce.4 = (f32[]{:T(128)}, f32[]{:T(128)}) all-reduce(f32[]{:T(128)} %get-tuple-element.28, f32[]{:T(128)} %get-tuple-element.29), channel_id=1, replica_groups=mesh['row_0'=4,'row_1'=2,'col_0'=4,'col_1'=4] {'col_0'}, use_global_device_ids=true, to_apply=%region_13.0 | all-reduce | flops 2 | bytes 16 | tf_op jit(solution)/shard_map/psum | solution.py:33
  236.0 12.5 %all-reduce.1 = (f32[]{:T(128)}, f32[]{:T(128)}) all-reduce(f32[]{:T(128)} %get-tuple-element.16, f32[]{:T(128)} %get-tuple-element.17), channel_id=1, replica_groups=mesh['row_0'=4,'row_1'=2,'col_0'=4,'col_1'=4] {'col_1'}, use_global_device_ids=true, to_apply=%region_14.0 | all-reduce | flops 2 | bytes 16 | tf_op jit(solution)/shard_map/psum | solution.py:33
  253.7 1.3 collective-permute-start.24
  255.0 1.3 collective-permute-start.25
  256.3 2.4 collective-permute-done.25
  258.8 1.9 collective-permute-start.26
  260.7 4.2 %collective-permute-start.27 = (f32[94,15]{1,0:T(8,128)S(1)}, f32[94,15]{1,0:T(8,128)S(1)}, u32[]{:S(2)}, u32[]{:S(2)}) collective-permute-start(f32[94,15]{1,0:T(8,128)S(1)} %get-tuple-element.104), channel_id=1, source_target_pairs={{1,0},{2,1},{3,2},{4,3},{5,4},{6,5},{7,6},{8,7},{9,8},{10,9},{11,1... | collective-permute-start | bytes 16928 | tf_op jit(solution)/shard_map/ppermute | solution.py:26
  265.0 1.9 collective-permute-done.27
  275.2 1.2 convolution_add_fusion.53
  283.6 1.3 collective-permute-start.29
  284.9 3.9 %collective-permute-start.28 = (f32[15,256]{1,0:T(8,128)S(1)}, f32[15,256]{1,0:T(8,128)S(1)}, u32[]{:S(2)}, u32[]{:S(2)}) collective-permute-start(f32[15,256]{1,0:T(8,128)S(1)} %bitcast.673), channel_id=1, source_target_pairs={{0,16},{16,32},{32,48},{48,64},{64,80},{80,96},{96,112},{1,17},{17... | collective-permute-start | bytes 46088 | tf_op jit(solution)/shard_map/ppermute | solution.py:25
  289.7 3.6 %collective-permute-start.31 = (f32[94,15]{1,0:T(8,128)S(1)}, f32[94,15]{1,0:T(8,128)S(1)}, u32[]{:S(2)}, u32[]{:S(2)}) collective-permute-start(f32[94,15]{1,0:T(8,128)S(1)} %get-tuple-element.99), channel_id=1, source_target_pairs={{1,0},{2,1},{3,2},{4,3},{5,4},{6,5},{7,6},{8,7},{9,8},{10,9},{11,1... | collective-permute-start | bytes 16928 | tf_op jit(solution)/shard_map/ppermute | solution.py:26
  293.4 2.4 collective-permute-start.30
  295.8 3.5 %collective-permute-done.30 = f32[94,15]{1,0:T(8,128)S(1)} collective-permute-done((f32[94,15]{1,0:T(8,128)S(1)}, f32[94,15]{1,0:T(8,128)S(1)}, u32[]{:S(2)}, u32[]{:S(2)}) %collective-permute-start.30) | collective-permute-done | bytes 5672 | tf_op jit(solution)/shard_map/ppermute | solution.py:25
  308.8 13.0 %all-reduce.6 = (f32[]{:T(128)}, f32[]{:T(128)}) all-reduce(f32[]{:T(128)} %get-tuple-element.3, f32[]{:T(128)} %get-tuple-element.2), channel_id=1, replica_groups=mesh['row_0'=4,'row_1'=2,'col_0'=4,'col_1'=4] {'row_0'}, use_global_device_ids=true, to_apply=%region_21.0 | all-reduce | flops 2 | bytes 16 | tf_op jit(solution)/shard_map/psum | solution.py:33
  321.8 3.2 all-reduce.9
  324.9 11.2 %all-reduce.3 = (f32[]{:T(128)}, f32[]{:T(128)}) all-reduce(f32[]{:T(128)} %get-tuple-element.26, f32[]{:T(128)} %get-tuple-element.27), channel_id=1, replica_groups=mesh['row_0'=4,'row_1'=2,'col_0'=4,'col_1'=4] {'col_0'}, use_global_device_ids=true, to_apply=%region_23.0 | all-reduce | flops 2 | bytes 16 | tf_op jit(solution)/shard_map/psum | solution.py:33
  336.1 12.5 %all-reduce = (f32[]{:T(128)}, f32[]{:T(128)}) all-reduce(f32[]{:T(128)} %get-tuple-element.14, f32[]{:T(128)} %get-tuple-element.15), channel_id=1, replica_groups=mesh['row_0'=4,'row_1'=2,'col_0'=4,'col_1'=4] {'col_1'}, use_global_device_ids=true, to_apply=%region_24.0 | all-reduce | flops 2 | bytes 16 | tf_op jit(solution)/shard_map/psum | solution.py:33
  (444 shorter events, 88.1 us)
Async XLA Ops:
  1.4 9.9 %collective-permute-start = (f32[15,256]{1,0:T(8,128)S(1)}, f32[15,256]{1,0:T(8,128)S(1)}, u32[]{:S(2)}, u32[]{:S(2)}) collective-permute-start(f32[15,256]{1,0:T(8,128)S(1)} %get-tuple-element.145), channel_id=1, source_target_pairs={{0,16},{16,32},{32,48},{48,64},{64,80},{80,96},{96,112},{1,17},{17... | collective-permute-start | bytes 46088 | tf_op jit(solution)/shard_map/ppermute | solution.py:25
  3.1 8.2 %collective-permute-start.1 = (f32[15,256]{1,0:T(8,128)S(1)}, f32[15,256]{1,0:T(8,128)S(1)}, u32[]{:S(2)}, u32[]{:S(2)}) collective-permute-start(f32[15,256]{1,0:T(8,128)S(1)} %get-tuple-element.146), channel_id=1, source_target_pairs={{16,0},{32,16},{48,32},{64,48},{80,64},{96,80},{112,96},{17,1},{33... | collective-permute-start | bytes 46088 | tf_op jit(solution)/shard_map/ppermute | solution.py:26
  11.4 7.3 %collective-permute-start.3 = (f32[94,15]{1,0:T(8,128)S(1)}, f32[94,15]{1,0:T(8,128)S(1)}, u32[]{:S(2)}, u32[]{:S(2)}) collective-permute-start(f32[94,15]{1,0:T(8,128)S(1)} %get-tuple-element.127), channel_id=1, source_target_pairs={{1,0},{2,1},{3,2},{4,3},{5,4},{6,5},{7,6},{8,7},{9,8},{10,9},{11,1... | collective-permute-start | bytes 16928 | tf_op jit(solution)/shard_map/ppermute | solution.py:26
  13.4 6.0 %collective-permute-start.2 = (f32[94,15]{1,0:T(8,128)S(1)}, f32[94,15]{1,0:T(8,128)S(1)}, u32[]{:S(2)}, u32[]{:S(2)}) collective-permute-start(f32[94,15]{1,0:T(8,128)S(1)} %get-tuple-element.128), channel_id=1, source_target_pairs={{0,1},{1,2},{2,3},{3,4},{4,5},{5,6},{6,7},{7,8},{8,9},{9,10},{10,1... | collective-permute-start | bytes 16928 | tf_op jit(solution)/shard_map/ppermute | solution.py:25
  18.6 54.9 %copy-start.44 = (f32[1,158,128]{2,0,1:T(1,128)}, f32[1,158,128]{2,0,1:T(1,128)S(1)}, u32[]{:S(2)}) copy-start(f32[1,158,128]{2,0,1:T(1,128)S(1)} %get-tuple-element.96) | copy-start | bytes 242692
  18.6 55.1 %copy-start.43 = (f32[1,158,128]{2,0,1:T(1,128)}, f32[1,158,128]{2,0,1:T(1,128)S(1)}, u32[]{:S(2)}) copy-start(f32[1,158,128]{2,0,1:T(1,128)S(1)} %get-tuple-element.95) | copy-start | bytes 242692
  18.6 55.4 %copy-start.42 = (f32[1,158,128]{2,0,1:T(1,128)}, f32[1,158,128]{2,0,1:T(1,128)S(1)}, u32[]{:S(2)}) copy-start(f32[1,158,128]{2,0,1:T(1,128)S(1)} %get-tuple-element.94) | copy-start | bytes 242692
  18.7 55.7 %copy-start.41 = (f32[1,158,128]{2,0,1:T(1,128)}, f32[1,158,128]{2,0,1:T(1,128)S(1)}, u32[]{:S(2)}) copy-start(f32[1,158,128]{2,0,1:T(1,128)S(1)} %get-tuple-element.93) | copy-start | bytes 242692
  18.7 56.0 %copy-start.40 = (f32[1,158,128]{2,0,1:T(1,128)}, f32[1,158,128]{2,0,1:T(1,128)S(1)}, u32[]{:S(2)}) copy-start(f32[1,158,128]{2,0,1:T(1,128)S(1)} %get-tuple-element.92) | copy-start | bytes 242692
  18.7 56.2 %copy-start.39 = (f32[1,158,128]{2,0,1:T(1,128)}, f32[1,158,128]{2,0,1:T(1,128)S(1)}, u32[]{:S(2)}) copy-start(f32[1,158,128]{2,0,1:T(1,128)S(1)} %get-tuple-element.91) | copy-start | bytes 242692
  18.7 56.5 %copy-start.38 = (f32[1,158,128]{2,0,1:T(1,128)}, f32[1,158,128]{2,0,1:T(1,128)S(1)}, u32[]{:S(2)}) copy-start(f32[1,158,128]{2,0,1:T(1,128)S(1)} %get-tuple-element.90) | copy-start | bytes 242692
  18.7 56.8 %copy-start.37 = (f32[1,158,128]{2,0,1:T(1,128)}, f32[1,158,128]{2,0,1:T(1,128)S(1)}, u32[]{:S(2)}) copy-start(f32[1,158,128]{2,0,1:T(1,128)S(1)} %get-tuple-element.89) | copy-start | bytes 242692
  18.7 57.0 %copy-start.33 = (f32[1,158,128]{2,0,1:T(1,128)}, f32[1,158,128]{2,0,1:T(1,128)S(1)}, u32[]{:S(2)}) copy-start(f32[1,158,128]{2,0,1:T(1,128)S(1)} %get-tuple-element.88) | copy-start | bytes 242692
  18.7 57.3 %copy-start.27 = (f32[1,158,128]{2,0,1:T(1,128)}, f32[1,158,128]{2,0,1:T(1,128)S(1)}, u32[]{:S(2)}) copy-start(f32[1,158,128]{2,0,1:T(1,128)S(1)} %get-tuple-element.87) | copy-start | bytes 242692
  18.7 57.6 %copy-start.21 = (f32[1,158,128]{2,0,1:T(1,128)}, f32[1,158,128]{2,0,1:T(1,128)S(1)}, u32[]{:S(2)}) copy-start(f32[1,158,128]{2,0,1:T(1,128)S(1)} %get-tuple-element.86) | copy-start | bytes 242692
  18.7 57.8 %copy-start.15 = (f32[1,158,128]{2,0,1:T(1,128)}, f32[1,158,128]{2,0,1:T(1,128)S(1)}, u32[]{:S(2)}) copy-start(f32[1,158,128]{2,0,1:T(1,128)S(1)} %get-tuple-element.85) | copy-start | bytes 242692
  28.0 5.8 %collective-permute-start.5 = (f32[15,256]{1,0:T(8,128)S(1)}, f32[15,256]{1,0:T(8,128)S(1)}, u32[]{:S(2)}, u32[]{:S(2)}) collective-permute-start(f32[15,256]{1,0:T(8,128)S(1)} %bitcast.677), channel_id=1, source_target_pairs={{16,0},{32,16},{48,32},{64,48},{80,64},{96,80},{112,96},{17,1},{33... | collective-permute-start | bytes 46088 | tf_op jit(solution)/shard_map/ppermute | solution.py:26
  29.3 5.3 %collective-permute-start.4 = (f32[15,256]{1,0:T(8,128)S(1)}, f32[15,256]{1,0:T(8,128)S(1)}, u32[]{:S(2)}, u32[]{:S(2)}) collective-permute-start(f32[15,256]{1,0:T(8,128)S(1)} %bitcast.674), channel_id=1, source_target_pairs={{0,16},{16,32},{32,48},{48,64},{64,80},{80,96},{96,112},{1,17},{17... | collective-permute-start | bytes 46088 | tf_op jit(solution)/shard_map/ppermute | solution.py:25
  34.7 6.9 %collective-permute-start.7 = (f32[94,15]{1,0:T(8,128)S(1)}, f32[94,15]{1,0:T(8,128)S(1)}, u32[]{:S(2)}, u32[]{:S(2)}) collective-permute-start(f32[94,15]{1,0:T(8,128)S(1)} %get-tuple-element.123), channel_id=1, source_target_pairs={{1,0},{2,1},{3,2},{4,3},{5,4},{6,5},{7,6},{8,7},{9,8},{10,9},{11,1... | collective-permute-start | bytes 16928 | tf_op jit(solution)/shard_map/ppermute | solution.py:26
  36.9 6.0 %collective-permute-start.6 = (f32[94,15]{1,0:T(8,128)S(1)}, f32[94,15]{1,0:T(8,128)S(1)}, u32[]{:S(2)}, u32[]{:S(2)}) collective-permute-start(f32[94,15]{1,0:T(8,128)S(1)} %get-tuple-element.124), channel_id=1, source_target_pairs={{0,1},{1,2},{2,3},{3,4},{4,5},{5,6},{6,7},{7,8},{8,9},{9,10},{10,1... | collective-permute-start | bytes 16928 | tf_op jit(solution)/shard_map/ppermute | solution.py:25
  41.5 56.9 %copy-start.34 = (f32[1,158,128]{2,0,1:T(1,128)}, f32[1,158,128]{2,0,1:T(1,128)S(1)}, u32[]{:S(2)}) copy-start(f32[1,158,128]{2,0,1:T(1,128)S(1)} %get-tuple-element.65) | copy-start | bytes 242692
  41.5 57.2 %copy-start.30 = (f32[1,158,128]{2,0,1:T(1,128)}, f32[1,158,128]{2,0,1:T(1,128)S(1)}, u32[]{:S(2)}) copy-start(f32[1,158,128]{2,0,1:T(1,128)S(1)} %get-tuple-element.64) | copy-start | bytes 242692
  41.5 57.4 %copy-start.24 = (f32[1,158,128]{2,0,1:T(1,128)}, f32[1,158,128]{2,0,1:T(1,128)S(1)}, u32[]{:S(2)}) copy-start(f32[1,158,128]{2,0,1:T(1,128)S(1)} %get-tuple-element.63) | copy-start | bytes 242692
  41.5 57.7 %copy-start.18 = (f32[1,158,128]{2,0,1:T(1,128)}, f32[1,158,128]{2,0,1:T(1,128)S(1)}, u32[]{:S(2)}) copy-start(f32[1,158,128]{2,0,1:T(1,128)S(1)} %get-tuple-element.62) | copy-start | bytes 242692
  41.5 58.0 %copy-start.12 = (f32[1,158,128]{2,0,1:T(1,128)}, f32[1,158,128]{2,0,1:T(1,128)S(1)}, u32[]{:S(2)}) copy-start(f32[1,158,128]{2,0,1:T(1,128)S(1)} %get-tuple-element.61) | copy-start | bytes 242692
  41.5 58.2 %copy-start.9 = (f32[1,158,128]{2,0,1:T(1,128)}, f32[1,158,128]{2,0,1:T(1,128)S(1)}, u32[]{:S(2)}) copy-start(f32[1,158,128]{2,0,1:T(1,128)S(1)} %get-tuple-element.60) | copy-start | bytes 242692
  41.5 58.5 %copy-start.6 = (f32[1,158,128]{2,0,1:T(1,128)}, f32[1,158,128]{2,0,1:T(1,128)S(1)}, u32[]{:S(2)}) copy-start(f32[1,158,128]{2,0,1:T(1,128)S(1)} %get-tuple-element.59) | copy-start | bytes 242692
  41.5 58.8 %copy-start.3 = (f32[1,158,128]{2,0,1:T(1,128)}, f32[1,158,128]{2,0,1:T(1,128)S(1)}, u32[]{:S(2)}) copy-start(f32[1,158,128]{2,0,1:T(1,128)S(1)} %get-tuple-element.58) | copy-start | bytes 242692
  41.5 59.0 %copy-start = (f32[1,158,128]{2,0,1:T(1,128)}, f32[1,158,128]{2,0,1:T(1,128)S(1)}, u32[]{:S(2)}) copy-start(f32[1,158,128]{2,0,1:T(1,128)S(1)} %get-tuple-element.57) | copy-start | bytes 242692
  51.5 5.0 %collective-permute-start.8 = (f32[15,256]{1,0:T(8,128)S(1)}, f32[15,256]{1,0:T(8,128)S(1)}, u32[]{:S(2)}, u32[]{:S(2)}) collective-permute-start(f32[15,256]{1,0:T(8,128)S(1)} %get-tuple-element.141), channel_id=1, source_target_pairs={{0,16},{16,32},{32,48},{48,64},{64,80},{80,96},{96,112},{1,17},{17... | collective-permute-start | bytes 46088 | tf_op jit(solution)/shard_map/ppermute | solution.py:25
  55.2 6.0 %collective-permute-start.9 = (f32[15,256]{1,0:T(8,128)S(1)}, f32[15,256]{1,0:T(8,128)S(1)}, u32[]{:S(2)}, u32[]{:S(2)}) collective-permute-start(f32[15,256]{1,0:T(8,128)S(1)} %get-tuple-element.142), channel_id=1, source_target_pairs={{16,0},{32,16},{48,32},{64,48},{80,64},{96,80},{112,96},{17,1},{33... | collective-permute-start | bytes 46088 | tf_op jit(solution)/shard_map/ppermute | solution.py:26
  61.3 6.1 %collective-permute-start.10 = (f32[94,15]{1,0:T(8,128)S(1)}, f32[94,15]{1,0:T(8,128)S(1)}, u32[]{:S(2)}, u32[]{:S(2)}) collective-permute-start(f32[94,15]{1,0:T(8,128)S(1)} %get-tuple-element.119), channel_id=1, source_target_pairs={{0,1},{1,2},{2,3},{3,4},{4,5},{5,6},{6,7},{7,8},{8,9},{9,10},{10,1... | collective-permute-start | bytes 16928 | tf_op jit(solution)/shard_map/ppermute | solution.py:25
  65.3 8.0 %collective-permute-start.11 = (f32[94,15]{1,0:T(8,128)S(1)}, f32[94,15]{1,0:T(8,128)S(1)}, u32[]{:S(2)}, u32[]{:S(2)}) collective-permute-start(f32[94,15]{1,0:T(8,128)S(1)} %get-tuple-element.120), channel_id=1, source_target_pairs={{1,0},{2,1},{3,2},{4,3},{5,4},{6,5},{7,6},{8,7},{9,8},{10,9},{11,1... | collective-permute-start | bytes 16928 | tf_op jit(solution)/shard_map/ppermute | solution.py:26
  82.1 5.2 %collective-permute-start.13 = (f32[15,256]{1,0:T(8,128)S(1)}, f32[15,256]{1,0:T(8,128)S(1)}, u32[]{:S(2)}, u32[]{:S(2)}) collective-permute-start(f32[15,256]{1,0:T(8,128)S(1)} %bitcast.678), channel_id=1, source_target_pairs={{16,0},{32,16},{48,32},{64,48},{80,64},{96,80},{112,96},{17,1},{33... | collective-permute-start | bytes 46088 | tf_op jit(solution)/shard_map/ppermute | solution.py:26
  83.4 4.7 %collective-permute-start.12 = (f32[15,256]{1,0:T(8,128)S(1)}, f32[15,256]{1,0:T(8,128)S(1)}, u32[]{:S(2)}, u32[]{:S(2)}) collective-permute-start(f32[15,256]{1,0:T(8,128)S(1)} %bitcast.675), channel_id=1, source_target_pairs={{0,16},{16,32},{32,48},{48,64},{64,80},{80,96},{96,112},{1,17},{17... | collective-permute-start | bytes 46088 | tf_op jit(solution)/shard_map/ppermute | solution.py:25
  88.1 8.6 %collective-permute-start.15 = (f32[94,15]{1,0:T(8,128)S(1)}, f32[94,15]{1,0:T(8,128)S(1)}, u32[]{:S(2)}, u32[]{:S(2)}) collective-permute-start(f32[94,15]{1,0:T(8,128)S(1)} %get-tuple-element.115), channel_id=1, source_target_pairs={{1,0},{2,1},{3,2},{4,3},{5,4},{6,5},{7,6},{8,7},{9,8},{10,9},{11,1... | collective-permute-start | bytes 16928 | tf_op jit(solution)/shard_map/ppermute | solution.py:26
  90.1 8.1 %collective-permute-start.14 = (f32[94,15]{1,0:T(8,128)S(1)}, f32[94,15]{1,0:T(8,128)S(1)}, u32[]{:S(2)}, u32[]{:S(2)}) collective-permute-start(f32[94,15]{1,0:T(8,128)S(1)} %get-tuple-element.116), channel_id=1, source_target_pairs={{0,1},{1,2},{2,3},{3,4},{4,5},{5,6},{6,7},{7,8},{8,9},{9,10},{10,1... | collective-permute-start | bytes 16928 | tf_op jit(solution)/shard_map/ppermute | solution.py:25
  107.6 70.8 %copy-start.47 = (f32[64,256]{1,0:T(8,128)}, f32[64,256]{1,0:T(8,128)S(1)}, u32[]{:S(2)}) copy-start(f32[64,256]{1,0:T(8,128)S(1)} %get-tuple-element.34) | copy-start | bytes 196612
  155.1 23.2 %copy-start.28 = (f32[1,158,128]{2,0,1:T(1,128)S(1)}, f32[1,158,128]{2,0,1:T(1,128)}, u32[]{:S(2)}) copy-start(f32[1,158,128]{2,0,1:T(1,128)} %copy-done.27) | copy-start | bytes 242692
  155.2 2.6 collective-permute-start.16
  156.5 3.1 collective-permute-start.17
  159.6 19.1 %copy-start.22 = (f32[1,158,128]{2,0,1:T(1,128)S(1)}, f32[1,158,128]{2,0,1:T(1,128)}, u32[]{:S(2)}) copy-start(f32[1,158,128]{2,0,1:T(1,128)} %copy-done.21) | copy-start | bytes 242692
  159.7 6.3 %collective-permute-start.18 = (f32[94,15]{1,0:T(8,128)S(1)}, f32[94,15]{1,0:T(8,128)S(1)}, u32[]{:S(2)}, u32[]{:S(2)}) collective-permute-start(f32[94,15]{1,0:T(8,128)S(1)} %get-tuple-element.111), channel_id=1, source_target_pairs={{0,1},{1,2},{2,3},{3,4},{4,5},{5,6},{6,7},{7,8},{8,9},{9,10},{10,1... | collective-permute-start | bytes 16928 | tf_op jit(solution)/shard_map/ppermute | solution.py:25
  161.6 6.1 %collective-permute-start.19 = (f32[94,15]{1,0:T(8,128)S(1)}, f32[94,15]{1,0:T(8,128)S(1)}, u32[]{:S(2)}, u32[]{:S(2)}) collective-permute-start(f32[94,15]{1,0:T(8,128)S(1)} %get-tuple-element.112), channel_id=1, source_target_pairs={{1,0},{2,1},{3,2},{4,3},{5,4},{6,5},{7,6},{8,7},{9,8},{10,9},{11,1... | collective-permute-start | bytes 16928 | tf_op jit(solution)/shard_map/ppermute | solution.py:26
  184.5 4.5 %collective-permute-start.21 = (f32[15,256]{1,0:T(8,128)S(1)}, f32[15,256]{1,0:T(8,128)S(1)}, u32[]{:S(2)}, u32[]{:S(2)}) collective-permute-start(f32[15,256]{1,0:T(8,128)S(1)} %bitcast.679), channel_id=1, source_target_pairs={{16,0},{32,16},{48,32},{64,48},{80,64},{96,80},{112,96},{17,1},{33... | collective-permute-start | bytes 46088 | tf_op jit(solution)/shard_map/ppermute | solution.py:26
  185.8 4.1 %collective-permute-start.20 = (f32[15,256]{1,0:T(8,128)S(1)}, f32[15,256]{1,0:T(8,128)S(1)}, u32[]{:S(2)}, u32[]{:S(2)}) collective-permute-start(f32[15,256]{1,0:T(8,128)S(1)} %bitcast.676), channel_id=1, source_target_pairs={{0,16},{16,32},{32,48},{48,64},{64,80},{80,96},{96,112},{1,17},{17... | collective-permute-start | bytes 46088 | tf_op jit(solution)/shard_map/ppermute | solution.py:25
  190.0 6.4 %collective-permute-start.23 = (f32[94,15]{1,0:T(8,128)S(1)}, f32[94,15]{1,0:T(8,128)S(1)}, u32[]{:S(2)}, u32[]{:S(2)}) collective-permute-start(f32[94,15]{1,0:T(8,128)S(1)} %get-tuple-element.107), channel_id=1, source_target_pairs={{1,0},{2,1},{3,2},{4,3},{5,4},{6,5},{7,6},{8,7},{9,8},{10,9},{11,1... | collective-permute-start | bytes 16928 | tf_op jit(solution)/shard_map/ppermute | solution.py:26
  193.7 6.1 %collective-permute-start.22 = (f32[94,15]{1,0:T(8,128)S(1)}, f32[94,15]{1,0:T(8,128)S(1)}, u32[]{:S(2)}, u32[]{:S(2)}) collective-permute-start(f32[94,15]{1,0:T(8,128)S(1)} %get-tuple-element.108), channel_id=1, source_target_pairs={{0,1},{1,2},{2,3},{3,4},{4,5},{5,6},{6,7},{7,8},{8,9},{9,10},{10,1... | collective-permute-start | bytes 16928 | tf_op jit(solution)/shard_map/ppermute | solution.py:25
  252.7 24.8 %copy-start.29 = (f32[1,158,128]{2,0,1:T(1,128)S(1)}, f32[1,158,128]{2,0,1:T(1,128)}, u32[]{:S(2)}) copy-start(f32[1,158,128]{2,0,1:T(1,128)} %copy-done.27) | copy-start | bytes 242692
  253.7 2.6 collective-permute-start.24
  255.0 3.7 %collective-permute-start.25 = (f32[15,256]{1,0:T(8,128)S(1)}, f32[15,256]{1,0:T(8,128)S(1)}, u32[]{:S(2)}, u32[]{:S(2)}) collective-permute-start(f32[15,256]{1,0:T(8,128)S(1)} %get-tuple-element.134), channel_id=1, source_target_pairs={{16,0},{32,16},{48,32},{64,48},{80,64},{96,80},{112,96},{17,1},{33... | collective-permute-start | bytes 46088 | tf_op jit(solution)/shard_map/ppermute | solution.py:26
  258.7 19.0 %copy-start.23 = (f32[1,158,128]{2,0,1:T(1,128)S(1)}, f32[1,158,128]{2,0,1:T(1,128)}, u32[]{:S(2)}) copy-start(f32[1,158,128]{2,0,1:T(1,128)} %copy-done.21) | copy-start | bytes 242692
  258.8 6.2 %collective-permute-start.26 = (f32[94,15]{1,0:T(8,128)S(1)}, f32[94,15]{1,0:T(8,128)S(1)}, u32[]{:S(2)}, u32[]{:S(2)}) collective-permute-start(f32[94,15]{1,0:T(8,128)S(1)} %get-tuple-element.103), channel_id=1, source_target_pairs={{0,1},{1,2},{2,3},{3,4},{4,5},{5,6},{6,7},{7,8},{8,9},{9,10},{10,1... | collective-permute-start | bytes 16928 | tf_op jit(solution)/shard_map/ppermute | solution.py:25
  260.7 6.1 %collective-permute-start.27 = (f32[94,15]{1,0:T(8,128)S(1)}, f32[94,15]{1,0:T(8,128)S(1)}, u32[]{:S(2)}, u32[]{:S(2)}) collective-permute-start(f32[94,15]{1,0:T(8,128)S(1)} %get-tuple-element.104), channel_id=1, source_target_pairs={{1,0},{2,1},{3,2},{4,3},{5,4},{6,5},{7,6},{8,7},{9,8},{10,9},{11,1... | collective-permute-start | bytes 16928 | tf_op jit(solution)/shard_map/ppermute | solution.py:26
  281.0 18.8 %copy-start.32 = (f32[1,158,128]{2,0,1:T(1,128)S(1)}, f32[1,158,128]{2,0,1:T(1,128)}, u32[]{:S(2)}) copy-start(f32[1,158,128]{2,0,1:T(1,128)} %copy-done.30) | copy-start | bytes 242692
  281.3 18.8 %copy-start.26 = (f32[1,158,128]{2,0,1:T(1,128)S(1)}, f32[1,158,128]{2,0,1:T(1,128)}, u32[]{:S(2)}) copy-start(f32[1,158,128]{2,0,1:T(1,128)} %copy-done.24) | copy-start | bytes 242692
  281.6 18.8 %copy-start.20 = (f32[1,158,128]{2,0,1:T(1,128)S(1)}, f32[1,158,128]{2,0,1:T(1,128)}, u32[]{:S(2)}) copy-start(f32[1,158,128]{2,0,1:T(1,128)} %copy-done.18) | copy-start | bytes 242692
  283.6 5.2 %collective-permute-start.29 = (f32[15,256]{1,0:T(8,128)S(1)}, f32[15,256]{1,0:T(8,128)S(1)}, u32[]{:S(2)}, u32[]{:S(2)}) collective-permute-start(f32[15,256]{1,0:T(8,128)S(1)} %bitcast.680), channel_id=1, source_target_pairs={{16,0},{32,16},{48,32},{64,48},{80,64},{96,80},{112,96},{17,1},{33... | collective-permute-start | bytes 46088 | tf_op jit(solution)/shard_map/ppermute | solution.py:26
  284.9 4.7 %collective-permute-start.28 = (f32[15,256]{1,0:T(8,128)S(1)}, f32[15,256]{1,0:T(8,128)S(1)}, u32[]{:S(2)}, u32[]{:S(2)}) collective-permute-start(f32[15,256]{1,0:T(8,128)S(1)} %bitcast.673), channel_id=1, source_target_pairs={{0,16},{16,32},{32,48},{48,64},{64,80},{80,96},{96,112},{1,17},{17... | collective-permute-start | bytes 46088 | tf_op jit(solution)/shard_map/ppermute | solution.py:25
  289.7 6.1 %collective-permute-start.31 = (f32[94,15]{1,0:T(8,128)S(1)}, f32[94,15]{1,0:T(8,128)S(1)}, u32[]{:S(2)}, u32[]{:S(2)}) collective-permute-start(f32[94,15]{1,0:T(8,128)S(1)} %get-tuple-element.99), channel_id=1, source_target_pairs={{1,0},{2,1},{3,2},{4,3},{5,4},{6,5},{7,6},{8,7},{9,8},{10,9},{11,1... | collective-permute-start | bytes 16928 | tf_op jit(solution)/shard_map/ppermute | solution.py:26
  293.4 6.0 %collective-permute-start.30 = (f32[94,15]{1,0:T(8,128)S(1)}, f32[94,15]{1,0:T(8,128)S(1)}, u32[]{:S(2)}, u32[]{:S(2)}) collective-permute-start(f32[94,15]{1,0:T(8,128)S(1)} %get-tuple-element.100), channel_id=1, source_target_pairs={{0,1},{1,2},{2,3},{3,4},{4,5},{5,6},{6,7},{7,8},{8,9},{9,10},{10,1... | collective-permute-start | bytes 16928 | tf_op jit(solution)/shard_map/ppermute | solution.py:25
  304.7 47.8 %copy-start.46 = (f32[64,256]{1,0:T(8,128)S(1)}, f32[64,256]{1,0:T(8,128)}, u32[]{:S(2)}) copy-start(f32[64,256]{1,0:T(8,128)} %param.4) | copy-start | bytes 196612
  304.7 47.8 %copy-start.48 = (f32[64,256]{1,0:T(8,128)S(1)}, f32[64,256]{1,0:T(8,128)}, u32[]{:S(2)}) copy-start(f32[64,256]{1,0:T(8,128)} %copy-done.47) | copy-start | bytes 196612
  304.7 47.8 %copy-start.49 = (f32[64,256]{1,0:T(8,128)S(1)}, f32[64,256]{1,0:T(8,128)}, u32[]{:S(2)}) copy-start(f32[64,256]{1,0:T(8,128)} %get-tuple-element.33) | copy-start | bytes 196612
  (19 other events, 318.2 us)
where the time goes:
time: 360 us; the launch traced here: 353 us
  blocking collectives  125 us (35%)
  starting transfers between devices  85.6 us (24%)
  matrix products  84.5 us (23%)
  waiting for transfers between devices  32 us (9%)
  between operations  13.5 us (4%)
  local copies, waits for them, and re-layouts  7.13 us (2%)
  other arithmetic  5.84 us (2%)
    psum x12, blocking collectives, one_axis_at_a_time(): x = lax.psum(x, axis)  125 us
    dot_general x248, matrix products, correlate(): jnp.einsum('rnk,kj->rnj', window, tables[shift_row], precision=lax.Precis...  81.1 us
    ppermute x16, starting transfers between devices, with_halo(): before = lax.ppermute(last, axis, up)  51.2 us
    ppermute x16, starting transfers between devices, with_halo(): after = lax.ppermute(initial, axis, down)  34.4 us
    ppermute x16, waiting for transfers between devices, with_halo(): after = lax.ppermute(initial, axis, down)  18.4 us
    ppermute x16, waiting for transfers between devices, with_halo(): before = lax.ppermute(last, axis, up)  13.6 us
  transfers between devices with their start and end apart: 32, of which 15 were waited for; matrix products, arithmetic and copies ran while one was open for 2% of the time, Pallas kernels for 0%

commit v1 on v0

v1 whole, which is shorter than its diff:
```python
import jax
import jax.numpy as jnp
from jax import lax
from jax.experimental import pallas as pl
from jax.experimental.pallas import tpu as pltpu
from jax.sharding import PartitionSpec as P

PENALTY = 0.05
F32, BF16 = jnp.float32, jnp.bfloat16
B = 16
LANES = B * B
PITCH = 24
ROWS = 13
FLAT = ROWS * PITCH
DIRECTIONS = ((-1, 0), (1, 0), (0, -1), (0, 1), (-1, -1), (-1, 1), (1, -1), (1, 1))
MESH = pl.DeviceIdType.MESH


def iota(shape, dim):
    return lax.broadcasted_iota(jnp.int32, shape, dim)


def roll(x, shift, axis):
    return pltpu.roll(x, shift % x.shape[axis], axis)


def split(x):
    high = x.astype(BF16)
    return high, (x - high.astype(F32)).astype(BF16)


def swap_blocks(x):
    top, bottom = [], []
    for i in range(4):
        upper, lower = x[16 * i : 16 * i + 8], x[16 * i + 8 : 16 * i + 16]
        top += [upper[:, :128], upper[:, 128:]]
        bottom += [lower[:, :128], lower[:, 128:]]
    y = jnp.concatenate(top + bottom, axis=0)
    row, lane = iota(y.shape, 0), iota(y.shape, 1)
    for t in range(3):
        step = 1 << t
        row_bit, lane_bit = (row >> t) & 1, (lane >> (t + 4)) & 1
        from_below = roll(roll(y, -step, 0), B * step, 1)
        from_above = roll(roll(y, step, 0), -B * step, 1)
        y = jnp.where(row_bit == lane_bit, y, jnp.where(row_bit == 0, from_below, from_above))
    return jnp.concatenate([y[:64], y[64:]], axis=1)


def build_weights(kernel_ref, padded_ref, shifted_ref, weights):
    padded_ref[...] = jnp.zeros_like(padded_ref)
    padded_ref[0:31, 0:31] = kernel_ref[...]
    taps = roll(padded_ref[...], 1, 1).T
    taps = taps[0:48]
    high, low = split(taps)
    flip = (iota((48, 48), 0) + iota((48, 48), 1) == 32).astype(F32).astype(BF16)
    flipped = [jnp.dot(flip, part, preferred_element_type=F32).astype(BF16) for part in (high, low)]
    lane_block = iota((128, 1024), 1) // B
    tap_row = iota((128, 1024), 0)
    spread = (tap_row == 46 - lane_block).astype(F32).astype(BF16)
    spread_flipped = (tap_row == lane_block - 16).astype(F32).astype(BF16)
    for number, (parts, selector) in enumerate((((high, low), spread), (tuple(flipped), spread_flipped))):
        base = jnp.dot(jnp.concatenate(parts, axis=0), selector, preferred_element_type=F32)
        column = iota(base.shape, 1) % B
        for t in range(4):
            base = jnp.where((column >> t) & 1 == 1, roll(base, 1 << t, 0), base)
        for shift in range(8):
            shifted_ref[shift] = roll(base, -B * shift, 1).astype(BF16)
        for part in range(2):
            weight = weights[2 * number + part]
            for di in (-1, 0, 1):
                for r in range(B):
                    start = 31 - 16 * di - r
                    lanes = 128 * (start // 8)
                    for dj in range(3):
                        rows = 48 * part + 16 * dj
                        weight[
                            LANES * (di + 1) + B * r : LANES * (di + 1) + B * r + B,
                            LANES * dj : LANES * dj + LANES,
                        ] = shifted_ref[start % 8, rows : rows + 16, lanes : lanes + LANES]


def correlate(source, high_weight, low_weight, first, count):
    highs, lows = [], []
    for di in (-1, 0, 1):
        high, low = split(source[pl.ds(first + PITCH * di, count), :])
        highs.append(high)
        lows.append(low)
    left = jnp.concatenate(highs + lows + highs, axis=1)
    right = jnp.concatenate([high_weight[...], high_weight[...], low_weight[...]], axis=0)
    y = jnp.dot(left, right, preferred_element_type=F32)
    return y[:, LANES : 2 * LANES] + roll(y[:, :LANES], 1, 0) + roll(y[:, 2 * LANES :], -1, 0)


def smooth(source, first, count):
    x = source[pl.ds(first, count), :]
    above = source[pl.ds(first - PITCH, count), :]
    below = source[pl.ds(first + PITCH, count), :]
    wide = source[pl.ds(first - 8, count + 16), :]
    before = roll(wide, 1, 0)[8 : 8 + count]
    after = roll(wide, -1, 0)[8 : 8 + count]
    lane = iota(x.shape, 1)
    column = lane % B
    upper = roll(jnp.where(lane >= LANES - B, above, x), B, 1)
    lower = roll(jnp.where(lane < B, below, x), -B, 1)
    leftward = jnp.where(column == 0, roll(before, -(B - 1), 1), roll(x, 1, 1))
    rightward = jnp.where(column == B - 1, roll(after, B - 1, 1), roll(x, -1, 1))
    return PENALTY * (4.0 * x - upper - lower - leftward - rightward)


def own(value, first):
    return jnp.concatenate(
        [value[PITCH * r + 8 - first : PITCH * r + 24 - first] for r in range(4, 8)], axis=0
    )


def pack_sides(middle, left_ref, right_ref):
    sublane = iota((8, LANES), 0)
    for pair in range(2):
        first, second = 4 + 2 * pair, 5 + 2 * pair
        left_ref[pair] = jnp.where(sublane < 4, middle[first, 0:8], roll(middle[second, 0:8], 4, 0))
        right_ref[pair] = jnp.where(sublane < 4, roll(middle[first, 8:16], 4, 0), middle[second, 8:16])


def unpack(middle, from_left, from_right, flat, masked):
    sublane = iota((8, LANES), 0)
    for r in range(ROWS):
        right = jnp.zeros((8, LANES), F32)
        left = right
        if r >= 1:
            right = from_right[(r - 1) // 2]
            if (r - 1) % 2:
                right = roll(right, 4, 0)
        if r < 12:
            left = from_left[r // 2]
            if r % 2 == 0:
                left = roll(left, 4, 0)
        start = PITCH * r
        flat[start : start + 8] = masked(jnp.where(sublane < 4, right, left), start, 8)
        if r < 12:
            flat[start + 8 : start + 24] = masked(middle[r], start + 8, 16)
        else:
            flat[start + 8 : start + 24] = jnp.zeros((16, LANES), F32)


def image_kernel(
    grid, b_ref, guess_ref, kernel_ref, template_ref, residual_ref,
    x_mid, v_mid, b_mid, x_left, x_right, v_left, v_right, b_left, b_right,
    x_from_left, x_from_right, v_from_left, v_from_right, b_from_left, b_from_right,
    xf, vf, bf, rf, t1, t2, mask_ref, padded_ref, shifted_ref, k_high, k_low, kt_high, kt_low,
    r0_own, v1_own, kr0_own, kv1_own, lr0_own, lv1_own,
    first_slots, second_slots,
    x_send, x_recv, b_send, b_recv, v_send, v_recv, first_send, first_recv, second_send, second_recv,
):
    n_rows, n_cols = grid
    row, col = lax.axis_index("row"), lax.axis_index("col")

    def at(dr, dc):
        return lax.rem(row + dr + n_rows, n_rows), lax.rem(col + dc + n_cols, n_cols)

    barrier = pltpu.get_barrier_semaphore()
    partners = [at(d, 0) for d in range(1, n_rows)] + [at(0, d) for d in range(1, n_cols)]
    partners += [at(dr, dc) for dr, dc in DIRECTIONS[4:]]
    for partner in partners:
        pl.semaphore_signal(barrier, inc=1, device_id=partner, device_id_type=MESH)

    def remote(source, target, send, recv, device):
        return pltpu.make_async_remote_copy(
            src_ref=source, dst_ref=target, send_sem=send, recv_sem=recv, device_id=device, device_id_type=MESH
        )

    def field_copies(middle, left, right, from_left, from_right, send, recv):
        copies = []
        for number, (dr, dc) in enumerate(DIRECTIONS):
            if dc == 0:
                source = middle.at[pl.ds(4, 4)]
                target = middle.at[pl.ds(4 - 4 * dr, 4)]
            else:
                source = right if dc == 1 else left
                target = (from_left if dc == 1 else from_right).at[pl.ds(2 - 2 * dr, 2)]
            copies.append(remote(source, target, send.at[number], recv.at[number], at(dr, dc)))
        return copies

    def spread(middle, first, x):
        for i in range(4):
            middle[first + i] = x[16 * i : 16 * i + 16]

    spread(x_mid, 4, swap_blocks(guess_ref[...]))
    pack_sides(x_mid, x_left, x_right)
    spread(b_mid, 2, swap_blocks(b_ref[...]))
    sublane = iota((8, LANES), 0)
    left_part = right_part = jnp.zeros((8, LANES), F32)
    for i in range(4):
        here = sublane // 2 == i
        left_part = jnp.where(here, roll(b_mid[2 + i, 0:8], 2 * i, 0), left_part)
        right_part = jnp.where(here, roll(b_mid[2 + i, 8:16], 2 * i + 2, 0), right_part)
    b_left[...] = left_part
    b_right[...] = right_part

    pl.semaphore_wait(barrier, n_rows - 1 + n_cols - 1 + 4)

    x_copies = field_copies(x_mid, x_left, x_right, x_from_left, x_from_right, x_send, x_recv)
    b_copies = []
    for number, (dr, dc) in enumerate(DIRECTIONS):
        if dc == 0:
            source = b_mid.at[pl.ds(2 if dr == -1 else 4, 2)]
            target = b_mid.at[pl.ds(6 if dr == -1 else 0, 2)]
        else:
            source = b_right if dc == 1 else b_left
            target = (b_from_left if dc == 1 else b_from_right).at[1 - dr]
        b_copies.append(remote(source, target, b_send.at[number], b_recv.at[number], at(dr, dc)))
    for copy in x_copies + b_copies:
        copy.start()

    build_weights(kernel_ref, padded_ref, shifted_ref, (k_high, k_low, kt_high, kt_low))
    flat = iota((FLAT, LANES), 0)
    slot = flat % PITCH
    block_row = row * 4 + flat // PITCH - 4 - (slot < 4).astype(jnp.int32)
    block_col = col * 16 + slot - 8 + 24 * (slot < 4).astype(jnp.int32)
    inside = (block_row >= 0) & (block_row < 4 * n_rows) & (block_col >= 0) & (block_col < 16 * n_cols)
    mask_ref[...] = inside.astype(F32)

    def masked(value, first, count):
        return jnp.where(mask_ref[pl.ds(first, count), :] > 0.5, value, 0.0)

    def apply_twice(source, second):
        t1[pl.ds(24, 256), :] = masked(correlate(source, k_high, k_low, 24, 256), 24, 256)
        blurred_source = own(t1[pl.ds(96, 112), :], 96)
        smooth_source = smooth(source, 48, 208)
        applied = correlate(t1, kt_high, kt_low, 48, 208) + smooth_source
        second[pl.ds(48, 208), :] = masked(bf[pl.ds(48, 208), :] - applied if source is xf else applied, 48, 208)
        blurred = correlate(second, k_high, k_low, 72, 160)
        t2[pl.ds(72, 160), :] = masked(blurred, 72, 160)
        return blurred_source, own(smooth_source, 48), own(blurred, 72), own(smooth(second, 96, 112), 96)

    for copy in x_copies:
        copy.wait_recv()
    unpack(x_mid, x_from_left, x_from_right, xf, masked)
    for copy in b_copies:
        copy.wait_recv()
    for r in range(2, 11):
        right = left = jnp.zeros((8, LANES), F32)
        if r >= 3:
            right = roll(b_from_right[(r - 1) // 4], -2 * ((r - 1) % 4), 0)
        if r < 10:
            left = roll(b_from_left[r // 4], 6 - 2 * (r % 4), 0)
        bf[PITCH * r : PITCH * r + 8] = jnp.where(sublane < 4, right, left)
        if r < 10:
            bf[PITCH * r + 8 : PITCH * r + 24] = b_mid[r - 2]

    _, _, kr0, lr0 = apply_twice(xf, rf)
    v1 = own(correlate(t2, kt_high, kt_low, 96, 112), 96) + lr0
    spread(v_mid, 4, v1)
    pack_sides(v_mid, v_left, v_right)
    v_copies = field_copies(v_mid, v_left, v_right, v_from_left, v_from_right, v_send, v_recv)
    for copy in v_copies:
        copy.start()
    r0_own[...] = own(rf[pl.ds(96, 112), :], 96)
    v1_own[...] = v1
    kr0_own[...] = kr0
    lr0_own[...] = lr0

    for copy in v_copies:
        copy.wait_recv()
    unpack(v_mid, v_from_left, v_from_right, vf, masked)
    kv1, lv1, kv2, lv2 = apply_twice(vf, rf)
    v2 = own(rf[pl.ds(96, 112), :], 96)

    def powers(zero, one, two):
        return two, one - two, zero - 2.0 * one + two

    r0, v1 = r0_own[...], v1_own[...]
    p = powers(r0, v1, v2)
    kp = powers(kr0_own[...], kv1, kv2)
    lp = powers(lr0_own[...], lv1, lv2)

    def lanes_of(x):
        total = x[0:8]
        for i in range(1, 8):
            total = total + x[8 * i : 8 * i + 8]
        total = total[:, :128] + total[:, 128:]
        return jnp.sum(total, axis=0, keepdims=True)

    moments = [lanes_of(p[2] * p[2])]
    for i, j in ((2, 2), (1, 2), (1, 1), (0, 1), (0, 0)):
        moments.append(lanes_of(kp[i] * kp[j] + p[i] * lp[j]))
    slot8 = iota((8, 128), 0)
    packed = jnp.zeros((8, 128), F32)
    for i, moment in enumerate(moments):
        packed = jnp.where(slot8 == i, moment, packed)

    def gather(slots, me, count, target, send, recv):
        return [
            remote(slots.at[me], slots.at[me], send.at[d - 1], recv.at[d - 1], target(d)) for d in range(1, count)
        ]

    first_slots[row] = packed
    first_copies = gather(first_slots, row, n_rows, lambda d: at(d, 0), first_send, first_recv)
    for copy in first_copies:
        copy.start()
    v3 = own(correlate(t2, kt_high, kt_low, 96, 112), 96) + lv2
    ap = powers(v1, v2, v3)
    for copy in first_copies:
        copy.wait_recv()
    total = first_slots[0]
    for i in range(1, n_rows):
        total = total + first_slots[i]
    second_slots[col] = total
    second_copies = gather(second_slots, col, n_cols, lambda d: at(0, d), second_send, second_recv)
    for copy in second_copies:
        copy.start()
    for copy in second_copies:
        copy.wait_recv()
    total = second_slots[0]
    for i in range(1, n_cols):
        total = total + second_slots[i]
    total = jnp.sum(total, axis=1, keepdims=True)
    b0, c1, c2, c3, c4, c5 = [total[i : i + 1, :] for i in range(6)]
    c = (None, c1, c2, c3, c4, c5)
    b = (b0, c1 + c2, c2 + c3, c3 + c4, c4 + c5)

    def square(q, m, base):
        return (
            q[0] * q[0] * m[base]
            + 2.0 * (q[0] * q[1]) * m[base + 1]
            + (q[1] * q[1] + 2.0 * (q[0] * q[2])) * m[base + 2]
            + 2.0 * (q[1] * q[2]) * m[base + 3]
            + q[2] * q[2] * m[base + 4]
        )

    def raised(q):
        return q[0], q[0] + q[1], q[1]

    one = (1.0, 2.0, 1.0)
    norm = square(one, b, 0)
    alpha0 = norm / square(one, c, 1)
    r1 = (1.0, 1.0 - alpha0)
    following = square(raised(r1), b, 0)
    beta0 = following / norm
    norm = following
    p1 = (r1[0] + beta0, r1[1] + beta0)
    p1_raised = raised(p1)
    alpha1 = norm / square(p1_raised, c, 1)
    r1_raised = raised(r1)
    r2 = (r1_raised[0], r1_raised[1] - alpha1 * p1[0], r1_raised[2] - alpha1 * p1[1])
    following = square(r2, b, 0)
    beta1 = following / norm
    p2 = tuple(r2[i] + beta1 * p1_raised[i] for i in range(3))
    alpha2 = following / square(p2, c, 1)
    steps = [alpha0 * one[i] + alpha1 * p1_raised[i] + alpha2 * p2[i] for i in range(3)]

    template = own(xf[pl.ds(96, 112), :], 96) + steps[0] * p[2] + steps[1] * p[1] + steps[2] * p[0]
    residual = r2[0] * p[2] + r2[1] * p[1] + r2[2] * p[0]
    residual = residual - alpha2 * (p2[0] * ap[2] + p2[1] * ap[1] + p2[2] * ap[0])
    template_ref[...] = swap_blocks(template)
    residual_ref[...] = swap_blocks(residual)
    for copy in x_copies + b_copies + v_copies + first_copies + second_copies:
        copy.wait_send()


def on_device(grid, right_side, initial_guess, kernel):
    n_rows, n_cols = grid
    middle = pltpu.VMEM((12, 16, LANES), F32)
    b_middle = pltpu.VMEM((8, 16, LANES), F32)
    side = pltpu.VMEM((2, 8, LANES), F32)
    halo = pltpu.VMEM((6, 8, LANES), F32)
    b_side = pltpu.VMEM((8, LANES), F32)
    b_halo = pltpu.VMEM((3, 8, LANES), F32)
    flat = pltpu.VMEM((FLAT, LANES), F32)
    weight = pltpu.VMEM((3 * LANES, 3 * LANES), BF16)
    tile = pltpu.VMEM((64, LANES), F32)
    dma = pltpu.SemaphoreType.DMA
    shape = jax.ShapeDtypeStruct((64, LANES), F32)
    vmem = pl.BlockSpec(memory_space=pltpu.VMEM)

    def body(*refs):
        image_kernel(grid, *refs)

    return pl.pallas_call(
        body,
        out_shape=(shape, shape),
        in_specs=[vmem] * 3,
        out_specs=(vmem, vmem),
        scratch_shapes=[
            middle, middle, b_middle, side, side, side, side, b_side, b_side,
            halo, halo, halo, halo, b_halo, b_halo,
            flat, flat, flat, flat, flat, flat, flat,
            pltpu.VMEM((128, 128), F32), pltpu.VMEM((8, 96, 1024), BF16),
            weight, weight, weight, weight,
            tile, tile, tile, tile, tile, tile,
            pltpu.VMEM((n_rows, 8, 128), F32), pltpu.VMEM((n_cols, 8, 128), F32),
            dma((8,)), dma((8,)), dma((8,)), dma((8,)), dma((8,)), dma((8,)),
            dma((n_rows - 1,)), dma((n_rows - 1,)), dma((n_cols - 1,)), dma((n_cols - 1,)),
        ],
        compiler_params=pltpu.CompilerParams(
            collective_id=0, has_side_effects=True, vmem_limit_bytes=48 * 1024 * 1024
        ),
    )(right_side, initial_guess, kernel)


def solution(mesh):
    grid = (mesh.shape["row"], mesh.shape["col"])
    tiles = P("row", "col")
    return jax.shard_map(
        lambda *arrays: on_device(grid, *arrays),
        mesh=mesh,
        in_specs=(tiles, tiles, P()),
        out_specs=(tiles, tiles),
        check_vma=False,
    )
```

time: 360 us -> 39.3 us (0.11)
  the two profiles are of different devices: /device:TPU:2 before, /device:TPU:1 now
where the time goes in v1:
time: 39.3 us; the launch traced here: 39.1 us
  Pallas kernels  34.8 us (89%)
  local copies, waits for them, and re-layouts  3.65 us (9%)
  between operations  0.65 us (2%)
    pallas_call x1, Pallas kernels, on_device(): pl.pallas_call(body, out_shape=(shape, shape), in_specs=[vmem] * 3, out_s...  34.8 us
    unnamed x8, local copies, waits for them, and re-layouts  3.65 us

profile of v1, /device:TPU:1, one launch (start us, length us, event | category | flops | bytes accessed | tf_op | source)
XLA Modules:
  0.0 39.1 jit_solution(15082842609262871632)
XLA Ops:
  0.6 0.0 copy-start
  0.6 0.8 %copy-done = f32[64,256]{1,0:T(8,128)S(1)} copy-done((f32[64,256]{1,0:T(8,128)S(1)}, f32[64,256]{1,0:T(8,128)}, u32[]{:S(2)}) %copy-start) | copy-done | bytes 65560
  1.5 0.0 copy-start.1
  1.5 0.8 %copy-done.1 = f32[64,256]{1,0:T(8,128)S(1)} copy-done((f32[64,256]{1,0:T(8,128)S(1)}, f32[64,256]{1,0:T(8,128)}, u32[]{:S(2)}) %copy-start.1) | copy-done | bytes 65560
  2.3 0.0 copy-start.2
  2.3 0.7 %copy-done.2 = f32[31,31]{1,0:T(8,128)S(1)} copy-done((f32[31,31]{1,0:T(8,128)S(1)}, f32[31,31]{1,0:T(8,128)}, u32[]{:S(2)}) %copy-start.2) | copy-done | bytes 3868
  3.0 34.8 %shard_map.50 = (f32[64,256]{1,0:T(8,128)S(1)}, f32[64,256]{1,0:T(8,128)S(1)}) custom-call(f32[64,256]{1,0:T(8,128)S(1)} %copy-done, f32[64,256]{1,0:T(8,128)S(1)} %copy-done.1, f32[31,31]{1,0:T(8,128)S(1)} %copy-done.2), custom_call_target="tpu_custom_call" | custom-call | tf_op jit(solution)/shard_map/pallas_call | solution.py:378
  37.8 0.6 %copy.7 = f32[64,256]{1,0:T(8,128)} copy(f32[64,256]{1,0:T(8,128)S(1)} %get-tuple-element.4) | data formatting | bytes 131072
  38.5 0.6 %copy.8 = f32[64,256]{1,0:T(8,128)} copy(f32[64,256]{1,0:T(8,128)S(1)} %get-tuple-element.5) | data formatting | bytes 131072
Async XLA Ops:
  0.6 0.8 %copy-start = (f32[64,256]{1,0:T(8,128)S(1)}, f32[64,256]{1,0:T(8,128)}, u32[]{:S(2)}) copy-start(f32[64,256]{1,0:T(8,128)} %refs_0_.1) | copy-start | bytes 196612
  1.5 0.8 %copy-start.1 = (f32[64,256]{1,0:T(8,128)S(1)}, f32[64,256]{1,0:T(8,128)}, u32[]{:S(2)}) copy-start(f32[64,256]{1,0:T(8,128)} %refs_1_.1) | copy-start | bytes 196612
  2.3 0.7 %copy-start.2 = (f32[31,31]{1,0:T(8,128)S(1)}, f32[31,31]{1,0:T(8,128)}, u32[]{:S(2)}) copy-start(f32[31,31]{1,0:T(8,128)} %refs_2_.1) | copy-start | bytes 11536

commit v2 on v1

--- a/solution.py
+++ b/solution.py
@@ -24,9 +24,14 @@
     return pltpu.roll(x, shift % x.shape[axis], axis)
 
 
-def split(x):
-    high = x.astype(BF16)
-    return high, (x - high.astype(F32)).astype(BF16)
+def rounded(x):
+    return x.astype(BF16).astype(F32)
+
+
+def put(pair, first, value):
+    rows = pl.ds(first, value.shape[0])
+    pair[0][rows, :] = value
+    pair[1][rows, :] = value - rounded(value)
 
 
 def swap_blocks(x):
@@ -46,25 +51,33 @@
     return jnp.concatenate([y[:64], y[64:]], axis=1)
 
 
-def build_weights(kernel_ref, padded_ref, shifted_ref, weights):
-    padded_ref[...] = jnp.zeros_like(padded_ref)
-    padded_ref[0:31, 0:31] = kernel_ref[...]
-    taps = roll(padded_ref[...], 1, 1).T
-    taps = taps[0:48]
-    high, low = split(taps)
-    flip = (iota((48, 48), 0) + iota((48, 48), 1) == 32).astype(F32).astype(BF16)
-    flipped = [jnp.dot(flip, part, preferred_element_type=F32).astype(BF16) for part in (high, low)]
-    lane_block = iota((128, 1024), 1) // B
-    tap_row = iota((128, 1024), 0)
-    spread = (tap_row == 46 - lane_block).astype(F32).astype(BF16)
-    spread_flipped = (tap_row == lane_block - 16).astype(F32).astype(BF16)
-    for number, (parts, selector) in enumerate((((high, low), spread), (tuple(flipped), spread_flipped))):
-        base = jnp.dot(jnp.concatenate(parts, axis=0), selector, preferred_element_type=F32)
+def pick_lanes(x, lanes):
+    return jnp.take_along_axis(x, lanes, axis=1, mode="promise_in_bounds")
+
+
+def build_weights(taps_ref, shifted_ref, weights):
+    taps = taps_ref[...]
+    lane = iota((128, 128), 1)
+    empty = (lane < 1) | (lane > 31)
+    ahead = jnp.where(empty, 0.0, roll(taps, 1, 1)).T[0:48]
+    flipped = jnp.where(empty, 0.0, pick_lanes(taps, jnp.clip(31 - lane, 0, 127))).T[0:48]
+    group = iota((48, 128), 1) // B
+    for number, source in enumerate((ahead, flipped)):
+        pieces = []
+        for tile in range(8):
+            block = 8 * tile + group
+            wanted = 46 - block if number == 0 else block - 16
+            valid = (wanted >= 0) & (wanted <= 30)
+            pieces.append(jnp.where(valid, pick_lanes(source, jnp.clip(wanted, 0, 30)), 0.0))
+        base = jnp.concatenate(pieces, axis=1)
         column = iota(base.shape, 1) % B
         for t in range(4):
             base = jnp.where((column >> t) & 1 == 1, roll(base, 1 << t, 0), base)
         for shift in range(8):
-            shifted_ref[shift] = roll(base, -B * shift, 1).astype(BF16)
+            moved = roll(base, -B * shift, 1)
+            high = moved.astype(BF16)
+            shifted_ref[shift, 0:48] = high
+            shifted_ref[shift, 48:96] = (moved - high.astype(F32)).astype(BF16)
         for part in range(2):
             weight = weights[2 * number + part]
             for di in (-1, 0, 1):
@@ -79,16 +92,35 @@
                         ] = shifted_ref[start % 8, rows : rows + 16, lanes : lanes + LANES]
 
 
-def correlate(source, high_weight, low_weight, first, count):
-    highs, lows = [], []
-    for di in (-1, 0, 1):
-        high, low = split(source[pl.ds(first + PITCH * di, count), :])
-        highs.append(high)
-        lows.append(low)
-    left = jnp.concatenate(highs + lows + highs, axis=1)
-    right = jnp.concatenate([high_weight[...], high_weight[...], low_weight[...]], axis=0)
-    y = jnp.dot(left, right, preferred_element_type=F32)
-    return y[:, LANES : 2 * LANES] + roll(y[:, :LANES], 1, 0) + roll(y[:, 2 * LANES :], -1, 0)
+FIRST_UNIT = [(di, 0, low) for low in (False, True) for di in (-1, 0, 1)] + [(-1, -1, False), (0, -1, False)]
+SECOND_UNIT = [(di, 1, low) for low in (False, True) for di in (-1, 0, 1)]
+SECOND_UNIT += [(1, -1, False), (-1, -1, True), (0, -1, True), (1, -1, True)]
+
+
+def correlate(field, high_weight, low_weight, first, count):
+    def body(middle, right, left0, left1):
+        queues = []
+        for unit, products in enumerate((FIRST_UNIT, SECOND_UNIT)):
+            queue = []
+            for number, (di, dj, low) in enumerate(products):
+                queue.append((unit, number % 2, di, dj, low, ((left0, left1)[unit], middle, right)[dj + 1]))
+            queues.append(queue)
+        for step in range(max(map(len, queues))):
+            for queue in queues:
+                if step < len(queue):
+                    unit, register, di, dj, low, total = queue[step]
+                    weight = low_weight if low else high_weight
+                    tile = weight[LANES * (di + 1) : LANES * (di + 2), LANES * (dj + 1) : LANES * (dj + 2)]
+                    pltpu.matmul_push_rhs(tile, staging_register=register, mxu_index=unit)
+                    rows = pl.ds(first + PITCH * di, count)
+                    pltpu.matmul_acc_lhs(total, field[0][rows, :], load_staged_rhs=register)
+                    if not low:
+                        pltpu.matmul_acc_lhs(total, field[1][rows, :])
+        value = pltpu.matmul_pop(middle) + roll(pltpu.matmul_pop(right), -1, 0)
+        return value + roll(pltpu.matmul_pop(left0) + pltpu.matmul_pop(left1), 1, 0)
+
+    totals = [pltpu.ACC(unit)((count, LANES), F32) for unit in (0, 1, 0, 1)]
+    return pl.run_scoped(body, *totals)
 
 
 def smooth(source, first, count):
@@ -135,23 +167,28 @@
             if r % 2 == 0:
                 left = roll(left, 4, 0)
         start = PITCH * r
-        flat[start : start + 8] = masked(jnp.where(sublane < 4, right, left), start, 8)
+        put(flat, start, masked(jnp.where(sublane < 4, right, left), start, 8))
         if r < 12:
-            flat[start + 8 : start + 24] = masked(middle[r], start + 8, 16)
+            put(flat, start + 8, masked(middle[r], start + 8, 16))
         else:
-            flat[start + 8 : start + 24] = jnp.zeros((16, LANES), F32)
+            put(flat, start + 8, jnp.zeros((16, LANES), F32))
 
 
 def image_kernel(
     grid, b_ref, guess_ref, kernel_ref, template_ref, residual_ref,
     x_mid, v_mid, b_mid, x_left, x_right, v_left, v_right, b_left, b_right,
     x_from_left, x_from_right, v_from_left, v_from_right, b_from_left, b_from_right,
-    xf, vf, bf, rf, t1, t2, mask_ref, padded_ref, shifted_ref, k_high, k_low, kt_high, kt_low,
+    xf, xf_low, vf, vf_low, bf, rf, rf_low, t1, t1_low, t2, t2_low, mask_ref, taps_ref, shifted_ref, k_high, k_low, kt_high, kt_low,
     r0_own, v1_own, kr0_own, kv1_own, lr0_own, lv1_own,
-    first_slots, second_slots,
+    first_slots, second_slots, guess_tile, b_tile, taps_in, in_sems,
     x_send, x_recv, b_send, b_recv, v_send, v_recv, first_send, first_recv, second_send, second_recv,
 ):
     n_rows, n_cols = grid
+    loads = (
+        pltpu.make_async_copy(guess_ref, guess_tile, in_sems.at[0]),
+        pltpu.make_async_copy(b_ref, b_tile, in_sems.at[1]),
+        pltpu.make_async_copy(kernel_ref, taps_in, in_sems.at[2]),
+    )
     row, col = lax.axis_index("row"), lax.axis_index("col")
 
     def at(dr, dc):
@@ -162,6 +199,10 @@
     partners += [at(dr, dc) for dr, dc in DIRECTIONS[4:]]
     for partner in partners:
         pl.semaphore_signal(barrier, inc=1, device_id=partner, device_id_type=MESH)
+
+    taps_ref[...] = jnp.zeros_like(taps_ref)
+    for load in loads:
+        load.start()
 
     def remote(source, target, send, recv, device):
         return pltpu.make_async_remote_copy(
@@ -184,9 +225,11 @@
         for i in range(4):
             middle[first + i] = x[16 * i : 16 * i + 16]
 
-    spread(x_mid, 4, swap_blocks(guess_ref[...]))
+    loads[0].wait()
+    spread(x_mid, 4, swap_blocks(guess_tile[...]))
     pack_sides(x_mid, x_left, x_right)
-    spread(b_mid, 2, swap_blocks(b_ref[...]))
+    loads[1].wait()
+    spread(b_mid, 2, swap_blocks(b_tile[...]))
     sublane = iota((8, LANES), 0)
     left_part = right_part = jnp.zeros((8, LANES), F32)
     for i in range(4):
@@ -211,7 +254,9 @@
     for copy in x_copies + b_copies:
         copy.start()
 
-    build_weights(kernel_ref, padded_ref, shifted_ref, (k_high, k_low, kt_high, kt_low))
+    loads[2].wait()
+    taps_ref[0:31, 0:31] = taps_in[...]
+    build_weights(taps_ref, shifted_ref, (k_high, k_low, kt_high, kt_low))
     flat = iota((FLAT, LANES), 0)
     slot = flat % PITCH
     block_row = row * 4 + flat // PITCH - 4 - (slot < 4).astype(jnp.int32)
@@ -223,18 +268,18 @@
         return jnp.where(mask_ref[pl.ds(first, count), :] > 0.5, value, 0.0)
 
     def apply_twice(source, second):
-        t1[pl.ds(24, 256), :] = masked(correlate(source, k_high, k_low, 24, 256), 24, 256)
+        put((t1, t1_low), 24, masked(correlate(source, k_high, k_low, 24, 256), 24, 256))
         blurred_source = own(t1[pl.ds(96, 112), :], 96)
-        smooth_source = smooth(source, 48, 208)
-        applied = correlate(t1, kt_high, kt_low, 48, 208) + smooth_source
-        second[pl.ds(48, 208), :] = masked(bf[pl.ds(48, 208), :] - applied if source is xf else applied, 48, 208)
-        blurred = correlate(second, k_high, k_low, 72, 160)
-        t2[pl.ds(72, 160), :] = masked(blurred, 72, 160)
-        return blurred_source, own(smooth_source, 48), own(blurred, 72), own(smooth(second, 96, 112), 96)
+        smooth_source = smooth(source[0], 48, 208)
+        applied = correlate((t1, t1_low), kt_high, kt_low, 48, 208) + smooth_source
+        put(second, 48, masked(bf[pl.ds(48, 208), :] - applied if source[0] is xf else applied, 48, 208))
+        blurred = masked(correlate(second, k_high, k_low, 72, 160), 72, 160)
+        put((t2, t2_low), 72, blurred)
+        return blurred_source, own(smooth_source, 48), own(blurred, 72), own(smooth(second[0], 96, 112), 96)
 
     for copy in x_copies:
         copy.wait_recv()
-    unpack(x_mid, x_from_left, x_from_right, xf, masked)
+    unpack(x_mid, x_from_left, x_from_right, (xf, xf_low), masked)
     for copy in b_copies:
         copy.wait_recv()
     for r in range(2, 11):
@@ -247,8 +292,8 @@
         if r < 10:
             bf[PITCH * r + 8 : PITCH * r + 24] = b_mid[r - 2]
 
-    _, _, kr0, lr0 = apply_twice(xf, rf)
-    v1 = own(correlate(t2, kt_high, kt_low, 96, 112), 96) + lr0
+    _, _, kr0, lr0 = apply_twice((xf, xf_low), (rf, rf_low))
+    v1 = own(correlate((t2, t2_low), kt_high, kt_low, 96, 112), 96) + lr0
     spread(v_mid, 4, v1)
     pack_sides(v_mid, v_left, v_right)
     v_copies = field_copies(v_mid, v_left, v_right, v_from_left, v_from_right, v_send, v_recv)
@@ -261,8 +306,8 @@
 
     for copy in v_copies:
         copy.wait_recv()
-    unpack(v_mid, v_from_left, v_from_right, vf, masked)
-    kv1, lv1, kv2, lv2 = apply_twice(vf, rf)
+    unpack(v_mid, v_from_left, v_from_right, (vf, vf_low), masked)
+    kv1, lv1, kv2, lv2 = apply_twice((vf, vf_low), (rf, rf_low))
     v2 = own(rf[pl.ds(96, 112), :], 96)
 
     def powers(zero, one, two):
@@ -297,7 +342,7 @@
     first_copies = gather(first_slots, row, n_rows, lambda d: at(d, 0), first_send, first_recv)
     for copy in first_copies:
         copy.start()
-    v3 = own(correlate(t2, kt_high, kt_low, 96, 112), 96) + lv2
+    v3 = own(correlate((t2, t2_low), kt_high, kt_low, 96, 112), 96) + lv2
     ap = powers(v1, v2, v3)
     for copy in first_copies:
         copy.wait_recv()
@@ -378,21 +423,21 @@
     return pl.pallas_call(
         body,
         out_shape=(shape, shape),
-        in_specs=[vmem] * 3,
+        in_specs=[pl.BlockSpec(memory_space=pl.ANY)] * 3,
         out_specs=(vmem, vmem),
         scratch_shapes=[
             middle, middle, b_middle, side, side, side, side, b_side, b_side,
             halo, halo, halo, halo, b_halo, b_halo,
-            flat, flat, flat, flat, flat, flat, flat,
+            flat, flat, flat, flat, flat, flat, flat, flat, flat, flat, flat, flat,
             pltpu.VMEM((128, 128), F32), pltpu.VMEM((8, 96, 1024), BF16),
             weight, weight, weight, weight,
             tile, tile, tile, tile, tile, tile,
-            pltpu.VMEM((n_rows, 8, 128), F32), pltpu.VMEM((n_cols, 8, 128), F32),
+            pltpu.VMEM((n_rows, 8, 128), F32), pltpu.VMEM((n_cols, 8, 128), F32), tile, tile, pltpu.VMEM((31, 31), F32), dma((3,)),
             dma((8,)), dma((8,)), dma((8,)), dma((8,)), dma((8,)), dma((8,)),
             dma((n_rows - 1,)), dma((n_rows - 1,)), dma((n_cols - 1,)), dma((n_cols - 1,)),
         ],
         compiler_params=pltpu.CompilerParams(
-            collective_id=0, has_side_effects=True, vmem_limit_bytes=48 * 1024 * 1024
+            collective_id=0, has_side_effects=True, vmem_limit_bytes=60 * 1024 * 1024
         ),
     )(right_side, initial_guess, kernel)
 

time: 39.3 us -> 37.8 us (0.962)
  local copies, waits for them, and re-layouts: 3.65 us -> 2.14 us
    unnamed x8 -> x4, local copies, waits for them, and re-layouts: 3.65 us -> 2.14 us
where the time goes in v2:
time: 37.8 us; the launch traced here: 37.6 us
  Pallas kernels  34.8 us (92%)
  local copies, waits for them, and re-layouts  2.14 us (6%)
  between operations  0.65 us (2%)
    pallas_call x1, Pallas kernels, on_device(): pl.pallas_call(body, out_shape=(shape, shape), in_specs=[pl.BlockSpec(mem...  34.8 us
    unnamed x4, local copies, waits for them, and re-layouts  2.14 us

profile of v2, /device:TPU:1, one launch (start us, length us, event | category | flops | bytes accessed | tf_op | source)
XLA Modules:
  0.0 37.6 jit_solution(1134387888391976638)
XLA Ops:
  0.6 34.8 %shard_map.50 = (f32[64,256]{1,0:T(8,128)}, f32[64,256]{1,0:T(8,128)}) custom-call(f32[64,256]{1,0:T(8,128)} %refs_0_.1, f32[64,256]{1,0:T(8,128)} %refs_1_.1, f32[31,31]{1,0:T(8,128)} %refs_2_.1), custom_call_target="tpu_custom_call" | custom-call | tf_op jit(solution)/shard_map/pallas_call | solution.py:423
  35.4 0.0 copy-start
  35.4 1.5 %copy.7 = f32[64,256]{1,0:T(8,128)} copy(f32[64,256]{1,0:T(8,128)} %get-tuple-element.4) | data formatting | bytes 131072
  36.9 0.0 copy-done
  36.9 0.6 %copy.8 = f32[64,256]{1,0:T(8,128)} copy(f32[64,256]{1,0:T(8,128)S(1)} %copy-done) | data formatting | bytes 131072
Async XLA Ops:
  35.4 1.5 %copy-start = (f32[64,256]{1,0:T(8,128)S(1)}, f32[64,256]{1,0:T(8,128)}, u32[]{:S(2)}) copy-start(f32[64,256]{1,0:T(8,128)} %get-tuple-element.5) | copy-start | bytes 196612

commit v3 on v2

--- a/solution.py
+++ b/solution.py
@@ -180,7 +180,7 @@
     x_from_left, x_from_right, v_from_left, v_from_right, b_from_left, b_from_right,
     xf, xf_low, vf, vf_low, bf, rf, rf_low, t1, t1_low, t2, t2_low, mask_ref, taps_ref, shifted_ref, k_high, k_low, kt_high, kt_low,
     r0_own, v1_own, kr0_own, kv1_own, lr0_own, lv1_own,
-    first_slots, second_slots, guess_tile, b_tile, taps_in, in_sems,
+    first_slots, second_slots, pixels, guess_tile, b_tile, taps_in, in_sems,
     x_send, x_recv, b_send, b_recv, v_send, v_recv, first_send, first_recv, second_send, second_recv,
 ):
     n_rows, n_cols = grid
@@ -268,14 +268,24 @@
         return jnp.where(mask_ref[pl.ds(first, count), :] > 0.5, value, 0.0)
 
     def apply_twice(source, second):
-        put((t1, t1_low), 24, masked(correlate(source, k_high, k_low, 24, 256), 24, 256))
-        blurred_source = own(t1[pl.ds(96, 112), :], 96)
-        smooth_source = smooth(source[0], 48, 208)
-        applied = correlate((t1, t1_low), kt_high, kt_low, 48, 208) + smooth_source
-        put(second, 48, masked(bf[pl.ds(48, 208), :] - applied if source[0] is xf else applied, 48, 208))
-        blurred = masked(correlate(second, k_high, k_low, 72, 160), 72, 160)
-        put((t2, t2_low), 72, blurred)
-        return blurred_source, own(smooth_source, 48), own(blurred, 72), own(smooth(second[0], 96, 112), 96)
+        for first, count, keep, kept in ((24, 152, 24, 144), (160, 112, 168, 104)):
+            value = correlate(source, k_high, k_low, first, count)[keep - first : keep - first + kept]
+            put((t1, t1_low), keep, masked(value, keep, kept))
+        smooth_source = []
+        for first, count, keep, kept in ((48, 104, 48, 96), (136, 112, 144, 104)):
+            value = correlate((t1, t1_low), kt_high, kt_low, first, count)[keep - first : keep - first + kept]
+            smooth_source.append(smooth(source[0], keep, kept))
+            value = value + smooth_source[-1]
+            put(second, keep, masked(bf[pl.ds(keep, kept), :] - value if source[0] is xf else value, keep, kept))
+        for first, count, keep, kept in ((72, 56, 72, 48), (112, 112, 120, 104)):
+            value = correlate(second, k_high, k_low, first, count)[keep - first : keep - first + kept]
+            put((t2, t2_low), keep, masked(value, keep, kept))
+        return (
+            own(t1[pl.ds(96, 104), :], 96),
+            own(jnp.concatenate(smooth_source, axis=0), 48),
+            own(t2[pl.ds(96, 104), :], 96),
+            own(smooth(second[0], 96, 104), 96),
+        )
 
     for copy in x_copies:
         copy.wait_recv()
@@ -293,13 +303,13 @@
             bf[PITCH * r + 8 : PITCH * r + 24] = b_mid[r - 2]
 
     _, _, kr0, lr0 = apply_twice((xf, xf_low), (rf, rf_low))
-    v1 = own(correlate((t2, t2_low), kt_high, kt_low, 96, 112), 96) + lr0
+    v1 = own(correlate((t2, t2_low), kt_high, kt_low, 96, 104), 96) + lr0
     spread(v_mid, 4, v1)
     pack_sides(v_mid, v_left, v_right)
     v_copies = field_copies(v_mid, v_left, v_right, v_from_left, v_from_right, v_send, v_recv)
     for copy in v_copies:
         copy.start()
-    r0_own[...] = own(rf[pl.ds(96, 112), :], 96)
+    r0_own[...] = own(rf[pl.ds(96, 104), :], 96)
     v1_own[...] = v1
     kr0_own[...] = kr0
     lr0_own[...] = lr0
@@ -308,7 +318,7 @@
         copy.wait_recv()
     unpack(v_mid, v_from_left, v_from_right, (vf, vf_low), masked)
     kv1, lv1, kv2, lv2 = apply_twice((vf, vf_low), (rf, rf_low))
-    v2 = own(rf[pl.ds(96, 112), :], 96)
+    v2 = own(rf[pl.ds(96, 104), :], 96)
 
     def powers(zero, one, two):
         return two, one - two, zero - 2.0 * one + two
@@ -332,6 +342,10 @@
     packed = jnp.zeros((8, 128), F32)
     for i, moment in enumerate(moments):
         packed = jnp.where(slot8 == i, moment, packed)
+    for step in (64, 32, 16):
+        packed = packed + roll(packed, step, 1)
+    mine = iota((8, 128), 1) // B == slot8
+    packed = jnp.sum(jnp.where(mine, packed, 0.0), axis=0, keepdims=True)
 
     def gather(slots, me, count, target, send, recv):
         return [
@@ -342,8 +356,9 @@
     first_copies = gather(first_slots, row, n_rows, lambda d: at(d, 0), first_send, first_recv)
     for copy in first_copies:
         copy.start()
-    v3 = own(correlate((t2, t2_low), kt_high, kt_low, 96, 112), 96) + lv2
-    ap = powers(v1, v2, v3)
+    v3 = own(correlate((t2, t2_low), kt_high, kt_low, 96, 104), 96) + lv2
+    for number, value in enumerate(p + powers(v1, v2, v3)):
+        pixels[number] = swap_blocks(value)
     for copy in first_copies:
         copy.wait_recv()
     total = first_slots[0]
@@ -358,7 +373,7 @@
     total = second_slots[0]
     for i in range(1, n_cols):
         total = total + second_slots[i]
-    total = jnp.sum(total, axis=1, keepdims=True)
+    total = jnp.sum(jnp.where(mine, jnp.broadcast_to(total, (8, 128)), 0.0), axis=1, keepdims=True)
     b0, c1, c2, c3, c4, c5 = [total[i : i + 1, :] for i in range(6)]
     c = (None, c1, c2, c3, c4, c5)
     b = (b0, c1 + c2, c2 + c3, c3 + c4, c4 + c5)
@@ -393,11 +408,10 @@
     alpha2 = following / square(p2, c, 1)
     steps = [alpha0 * one[i] + alpha1 * p1_raised[i] + alpha2 * p2[i] for i in range(3)]
 
-    template = own(xf[pl.ds(96, 112), :], 96) + steps[0] * p[2] + steps[1] * p[1] + steps[2] * p[0]
-    residual = r2[0] * p[2] + r2[1] * p[1] + r2[2] * p[0]
-    residual = residual - alpha2 * (p2[0] * ap[2] + p2[1] * ap[1] + p2[2] * ap[0])
-    template_ref[...] = swap_blocks(template)
-    residual_ref[...] = swap_blocks(residual)
+    f0, f1, f2, af0, af1, af2 = [pixels[number] for number in range(6)]
+    template_ref[...] = guess_tile[...] + steps[0] * f2 + steps[1] * f1 + steps[2] * f0
+    residual = r2[0] * f2 + r2[1] * f1 + r2[2] * f0
+    residual_ref[...] = residual - alpha2 * (p2[0] * af2 + p2[1] * af1 + p2[2] * af0)
     for copy in x_copies + b_copies + v_copies + first_copies + second_copies:
         copy.wait_send()
 
@@ -423,7 +437,7 @@
     return pl.pallas_call(
         body,
         out_shape=(shape, shape),
-        in_specs=[pl.BlockSpec(memory_space=pl.ANY)] * 3,
+        in_specs=[pl.BlockSpec(memory_space=pltpu.HBM)] * 3,
         out_specs=(vmem, vmem),
         scratch_shapes=[
             middle, middle, b_middle, side, side, side, side, b_side, b_side,
@@ -432,14 +446,14 @@
             pltpu.VMEM((128, 128), F32), pltpu.VMEM((8, 96, 1024), BF16),
             weight, weight, weight, weight,
             tile, tile, tile, tile, tile, tile,
-            pltpu.VMEM((n_rows, 8, 128), F32), pltpu.VMEM((n_cols, 8, 128), F32), tile, tile, pltpu.VMEM((31, 31), F32), dma((3,)),
+            pltpu.VMEM((n_rows, 1, 128), F32), pltpu.VMEM((n_cols, 1, 128), F32), pltpu.VMEM((6, 64, LANES), F32), tile, tile, pltpu.VMEM((31, 31), F32), dma((3,)),
             dma((8,)), dma((8,)), dma((8,)), dma((8,)), dma((8,)), dma((8,)),
             dma((n_rows - 1,)), dma((n_rows - 1,)), dma((n_cols - 1,)), dma((n_cols - 1,)),
         ],
         compiler_params=pltpu.CompilerParams(
-            collective_id=0, has_side_effects=True, vmem_limit_bytes=60 * 1024 * 1024
+            collective_id=0, has_side_effects=True, vmem_limit_bytes=16 * 1024 * 1024
         ),
-    )(right_side, initial_guess, kernel)
+    )(*(pltpu.with_memory_space_constraint(x, pltpu.HBM) for x in (right_side, initial_guess, kernel)))
 
 
 def solution(mesh):

time: 37.8 us -> 36.4 us (0.963)
  local copies, waits for them, and re-layouts: 2.14 us -> 1.26 us
  Pallas kernels: 34.8 us -> 34.2 us
    unnamed x4 -> x2, local copies, waits for them, and re-layouts: 2.14 us -> 1.26 us
    pallas_call x1, Pallas kernels: 34.8 us -> 34.2 us  [on_device(): pl.pallas_call(body, out_shape=(shape, shape), in_specs=[pl.BlockSpec(mem...]
where the time goes in v3:
time: 36.4 us; the launch traced here: 36.1 us
  Pallas kernels  34.2 us (94%)
  local copies, waits for them, and re-layouts  1.26 us (3%)
  between operations  0.64 us (2%)
    pallas_call x1, Pallas kernels, on_device(): pl.pallas_call(body, out_shape=(shape, shape), in_specs=[pl.BlockSpec(mem...  34.2 us
    unnamed x2, local copies, waits for them, and re-layouts  1.26 us

profile of v3, /device:TPU:1, one launch (start us, length us, event | category | flops | bytes accessed | tf_op | source)
XLA Modules:
  0.0 36.1 jit_solution(7275020507691319226)
XLA Ops:
  0.6 34.2 %shard_map.50 = (f32[64,256]{1,0:T(8,128)S(1)}, f32[64,256]{1,0:T(8,128)S(1)}) custom-call(f32[64,256]{1,0:T(8,128)} %refs_0_.1, f32[64,256]{1,0:T(8,128)} %refs_1_.1, f32[31,31]{1,0:T(8,128)} %refs_2_.1), custom_call_target="tpu_custom_call" | custom-call | tf_op jit(solution)/shard_map/pallas_call | solution.py:437
  34.8 0.6 %copy.7 = f32[64,256]{1,0:T(8,128)} copy(f32[64,256]{1,0:T(8,128)S(1)} %get-tuple-element.4) | data formatting | bytes 131072
  35.5 0.6 %copy.8 = f32[64,256]{1,0:T(8,128)} copy(f32[64,256]{1,0:T(8,128)S(1)} %get-tuple-element.5) | data formatting | bytes 131072

commit v4 on v3

--- a/solution.py
+++ b/solution.py
@@ -12,7 +12,7 @@
 PITCH = 24
 ROWS = 13
 FLAT = ROWS * PITCH
-DIRECTIONS = ((-1, 0), (1, 0), (0, -1), (0, 1), (-1, -1), (-1, 1), (1, -1), (1, 1))
+DIRECTIONS = ((-1, -1), (-1, 1), (1, -1), (1, 1), (0, -1), (0, 1), (-1, 0), (1, 0))
 MESH = pl.DeviceIdType.MESH
 
 
@@ -180,7 +180,7 @@
     x_from_left, x_from_right, v_from_left, v_from_right, b_from_left, b_from_right,
     xf, xf_low, vf, vf_low, bf, rf, rf_low, t1, t1_low, t2, t2_low, mask_ref, taps_ref, shifted_ref, k_high, k_low, kt_high, kt_low,
     r0_own, v1_own, kr0_own, kv1_own, lr0_own, lv1_own,
-    first_slots, second_slots, pixels, guess_tile, b_tile, taps_in, in_sems,
+    first_slots, second_slots, pixels, far_sems, guess_tile, b_tile, taps_in, in_sems,
     x_send, x_recv, b_send, b_recv, v_send, v_recv, first_send, first_recv, second_send, second_recv,
 ):
     n_rows, n_cols = grid
@@ -194,15 +194,12 @@
     def at(dr, dc):
         return lax.rem(row + dr + n_rows, n_rows), lax.rem(col + dc + n_cols, n_cols)
 
+    for load in loads:
+        load.start()
     barrier = pltpu.get_barrier_semaphore()
-    partners = [at(d, 0) for d in range(1, n_rows)] + [at(0, d) for d in range(1, n_cols)]
-    partners += [at(dr, dc) for dr, dc in DIRECTIONS[4:]]
+    partners = [at(dr, dc) for dr, dc in DIRECTIONS[:6]] + [at(d, 0) for d in range(1, n_rows)]
     for partner in partners:
         pl.semaphore_signal(barrier, inc=1, device_id=partner, device_id_type=MESH)
-
-    taps_ref[...] = jnp.zeros_like(taps_ref)
-    for load in loads:
-        load.start()
 
     def remote(source, target, send, recv, device):
         return pltpu.make_async_remote_copy(
@@ -228,6 +225,11 @@
     loads[0].wait()
     spread(x_mid, 4, swap_blocks(guess_tile[...]))
     pack_sides(x_mid, x_left, x_right)
+    pl.semaphore_wait(barrier, n_rows - 1 + 6)
+
+    x_copies = field_copies(x_mid, x_left, x_right, x_from_left, x_from_right, x_send, x_recv)
+    for copy in x_copies:
+        copy.start()
     loads[1].wait()
     spread(b_mid, 2, swap_blocks(b_tile[...]))
     sublane = iota((8, LANES), 0)
@@ -239,9 +241,6 @@
     b_left[...] = left_part
     b_right[...] = right_part
 
-    pl.semaphore_wait(barrier, n_rows - 1 + n_cols - 1 + 4)
-
-    x_copies = field_copies(x_mid, x_left, x_right, x_from_left, x_from_right, x_send, x_recv)
     b_copies = []
     for number, (dr, dc) in enumerate(DIRECTIONS):
         if dc == 0:
@@ -251,9 +250,10 @@
             source = b_right if dc == 1 else b_left
             target = (b_from_left if dc == 1 else b_from_right).at[1 - dr]
         b_copies.append(remote(source, target, b_send.at[number], b_recv.at[number], at(dr, dc)))
-    for copy in x_copies + b_copies:
+    for copy in b_copies:
         copy.start()
 
+    taps_ref[...] = jnp.zeros_like(taps_ref)
     loads[2].wait()
     taps_ref[0:31, 0:31] = taps_in[...]
     build_weights(taps_ref, shifted_ref, (k_high, k_low, kt_high, kt_low))
@@ -267,10 +267,37 @@
     def masked(value, first, count):
         return jnp.where(mask_ref[pl.ds(first, count), :] > 0.5, value, 0.0)
 
-    def apply_twice(source, second):
+    distances = []
+    while 2 << len(distances) < n_cols // 2:
+        distances.append(2 << len(distances))
+
+    def greet(number):
+        if number < len(distances):
+            for d in (distances[number], n_cols - distances[number]):
+                pl.semaphore_signal(far_sems.at[number], inc=1, device_id=at(0, d), device_id_type=MESH)
+
+    def meet(number):
+        if number < len(distances):
+            pl.semaphore_wait(far_sems.at[number], 2)
+
+    def take_b():
+        for copy in b_copies:
+            copy.wait_recv()
+        for r in range(2, 11):
+            right = left = jnp.zeros((8, LANES), F32)
+            if r >= 3:
+                right = roll(b_from_right[(r - 1) // 4], -2 * ((r - 1) % 4), 0)
+            if r < 10:
+                left = roll(b_from_left[r // 4], 6 - 2 * (r % 4), 0)
+            bf[PITCH * r : PITCH * r + 8] = jnp.where(sublane < 4, right, left)
+            if r < 10:
+                bf[PITCH * r + 8 : PITCH * r + 24] = b_mid[r - 2]
+
+    def apply_twice(source, second, between):
         for first, count, keep, kept in ((24, 152, 24, 144), (160, 112, 168, 104)):
             value = correlate(source, k_high, k_low, first, count)[keep - first : keep - first + kept]
             put((t1, t1_low), keep, masked(value, keep, kept))
+        between()
         smooth_source = []
         for first, count, keep, kept in ((48, 104, 48, 96), (136, 112, 144, 104)):
             value = correlate((t1, t1_low), kt_high, kt_low, first, count)[keep - first : keep - first + kept]
@@ -289,26 +316,17 @@
 
     for copy in x_copies:
         copy.wait_recv()
+    greet(0)
     unpack(x_mid, x_from_left, x_from_right, (xf, xf_low), masked)
-    for copy in b_copies:
-        copy.wait_recv()
-    for r in range(2, 11):
-        right = left = jnp.zeros((8, LANES), F32)
-        if r >= 3:
-            right = roll(b_from_right[(r - 1) // 4], -2 * ((r - 1) % 4), 0)
-        if r < 10:
-            left = roll(b_from_left[r // 4], 6 - 2 * (r % 4), 0)
-        bf[PITCH * r : PITCH * r + 8] = jnp.where(sublane < 4, right, left)
-        if r < 10:
-            bf[PITCH * r + 8 : PITCH * r + 24] = b_mid[r - 2]
-
-    _, _, kr0, lr0 = apply_twice((xf, xf_low), (rf, rf_low))
+    _, _, kr0, lr0 = apply_twice((xf, xf_low), (rf, rf_low), take_b)
     v1 = own(correlate((t2, t2_low), kt_high, kt_low, 96, 104), 96) + lr0
     spread(v_mid, 4, v1)
     pack_sides(v_mid, v_left, v_right)
     v_copies = field_copies(v_mid, v_left, v_right, v_from_left, v_from_right, v_send, v_recv)
     for copy in v_copies:
         copy.start()
+    meet(0)
+    greet(1)
     r0_own[...] = own(rf[pl.ds(96, 104), :], 96)
     v1_own[...] = v1
     kr0_own[...] = kr0
@@ -317,7 +335,7 @@
     for copy in v_copies:
         copy.wait_recv()
     unpack(v_mid, v_from_left, v_from_right, (vf, vf_low), masked)
-    kv1, lv1, kv2, lv2 = apply_twice((vf, vf_low), (rf, rf_low))
+    kv1, lv1, kv2, lv2 = apply_twice((vf, vf_low), (rf, rf_low), lambda: None)
     v2 = own(rf[pl.ds(96, 104), :], 96)
 
     def powers(zero, one, two):
@@ -361,6 +379,7 @@
         pixels[number] = swap_blocks(value)
     for copy in first_copies:
         copy.wait_recv()
+    meet(1)
     total = first_slots[0]
     for i in range(1, n_rows):
         total = total + first_slots[i]
@@ -446,7 +465,7 @@
             pltpu.VMEM((128, 128), F32), pltpu.VMEM((8, 96, 1024), BF16),
             weight, weight, weight, weight,
             tile, tile, tile, tile, tile, tile,
-            pltpu.VMEM((n_rows, 1, 128), F32), pltpu.VMEM((n_cols, 1, 128), F32), pltpu.VMEM((6, 64, LANES), F32), tile, tile, pltpu.VMEM((31, 31), F32), dma((3,)),
+            pltpu.VMEM((n_rows, 1, 128), F32), pltpu.VMEM((n_cols, 1, 128), F32), pltpu.VMEM((6, 64, LANES), F32), pltpu.SemaphoreType.REGULAR((2,)), tile, tile, pltpu.VMEM((31, 31), F32), dma((3,)),
             dma((8,)), dma((8,)), dma((8,)), dma((8,)), dma((8,)), dma((8,)),
             dma((n_rows - 1,)), dma((n_rows - 1,)), dma((n_cols - 1,)), dma((n_cols - 1,)),
         ],

time: 36.4 us -> 36.1 us (level)
  no operation moved by 1% of the time
where the time goes in v4:
time: 36.1 us; the launch traced here: 35.8 us
  Pallas kernels  33.9 us (94%)
  local copies, waits for them, and re-layouts  1.26 us (3%)
  between operations  0.64 us (2%)
    pallas_call x1, Pallas kernels, on_device(): pl.pallas_call(body, out_shape=(shape, shape), in_specs=[pl.BlockSpec(mem...  33.9 us
    unnamed x2, local copies, waits for them, and re-layouts  1.26 us

profile of v4, /device:TPU:1, one launch (start us, length us, event | category | flops | bytes accessed | tf_op | source)
XLA Modules:
  0.0 35.8 jit_solution(7784985004779715029)
XLA Ops:
  0.6 33.9 %shard_map.50 = (f32[64,256]{1,0:T(8,128)S(1)}, f32[64,256]{1,0:T(8,128)S(1)}) custom-call(f32[64,256]{1,0:T(8,128)} %refs_0_.1, f32[64,256]{1,0:T(8,128)} %refs_1_.1, f32[31,31]{1,0:T(8,128)} %refs_2_.1), custom_call_target="tpu_custom_call" | custom-call | tf_op jit(solution)/shard_map/pallas_call | solution.py:456
  34.5 0.6 %copy.7 = f32[64,256]{1,0:T(8,128)} copy(f32[64,256]{1,0:T(8,128)S(1)} %get-tuple-element.4) | data formatting | bytes 131072
  35.1 0.6 %copy.8 = f32[64,256]{1,0:T(8,128)} copy(f32[64,256]{1,0:T(8,128)S(1)} %get-tuple-element.5) | data formatting | bytes 131072

commit v5 on v4

--- a/solution.py
+++ b/solution.py
@@ -180,8 +180,8 @@
     x_from_left, x_from_right, v_from_left, v_from_right, b_from_left, b_from_right,
     xf, xf_low, vf, vf_low, bf, rf, rf_low, t1, t1_low, t2, t2_low, mask_ref, taps_ref, shifted_ref, k_high, k_low, kt_high, kt_low,
     r0_own, v1_own, kr0_own, kv1_own, lr0_own, lv1_own,
-    first_slots, second_slots, pixels, far_sems, guess_tile, b_tile, taps_in, in_sems,
-    x_send, x_recv, b_send, b_recv, v_send, v_recv, first_send, first_recv, second_send, second_recv,
+    slots, pixels, far_sems, guess_tile, b_tile, taps_in, in_sems,
+    x_send, x_recv, b_send, b_recv, v_send, v_recv, sum_send, sum_recv,
 ):
     n_rows, n_cols = grid
     loads = (
@@ -268,17 +268,17 @@
         return jnp.where(mask_ref[pl.ds(first, count), :] > 0.5, value, 0.0)
 
     distances = []
-    while 2 << len(distances) < n_cols // 2:
+    while 2 << len(distances) <= n_cols // 2:
         distances.append(2 << len(distances))
 
     def greet(number):
         if number < len(distances):
-            for d in (distances[number], n_cols - distances[number]):
+            for d in sorted({distances[number], n_cols - distances[number]}):
                 pl.semaphore_signal(far_sems.at[number], inc=1, device_id=at(0, d), device_id_type=MESH)
 
     def meet(number):
         if number < len(distances):
-            pl.semaphore_wait(far_sems.at[number], 2)
+            pl.semaphore_wait(far_sems.at[number], 1 if 2 * distances[number] == n_cols else 2)
 
     def take_b():
         for copy in b_copies:
@@ -334,6 +334,8 @@
 
     for copy in v_copies:
         copy.wait_recv()
+    meet(1)
+    greet(2)
     unpack(v_mid, v_from_left, v_from_right, (vf, vf_low), masked)
     kv1, lv1, kv2, lv2 = apply_twice((vf, vf_low), (rf, rf_low), lambda: None)
     v2 = own(rf[pl.ds(96, 104), :], 96)
@@ -360,38 +362,30 @@
     packed = jnp.zeros((8, 128), F32)
     for i, moment in enumerate(moments):
         packed = jnp.where(slot8 == i, moment, packed)
-    for step in (64, 32, 16):
-        packed = packed + roll(packed, step, 1)
-    mine = iota((8, 128), 1) // B == slot8
+    mine = iota((8, 128), 1) == slot8
+    packed = jnp.sum(packed, axis=1, keepdims=True)
     packed = jnp.sum(jnp.where(mine, packed, 0.0), axis=0, keepdims=True)
 
-    def gather(slots, me, count, target, send, recv):
-        return [
-            remote(slots.at[me], slots.at[me], send.at[d - 1], recv.at[d - 1], target(d)) for d in range(1, count)
-        ]
-
-    first_slots[row] = packed
-    first_copies = gather(first_slots, row, n_rows, lambda d: at(d, 0), first_send, first_recv)
-    for copy in first_copies:
-        copy.start()
+    meet(2)
+    me = row * n_cols + col
+    slots[me] = packed
+
+    def hops(offset):
+        z, y, x = offset[0] // 2, offset[1] // 4, offset[1] % 4
+        return -(min(z, 4 - z) + min(y, 4 - y) + min(x, 4 - x))
+
+    rows_at = [at(d, 0)[0] for d in range(n_rows)]
+    cols_at = [at(0, d)[1] for d in range(n_cols)]
+    offsets = [(dr, dc) for dr in range(n_rows) for dc in range(n_cols)][1:]
+    for dr, dc in sorted(offsets, key=hops):
+        remote(slots.at[me], slots.at[me], sum_send, sum_recv, (rows_at[dr], cols_at[dc])).start()
+    others = pl.ds(0, n_rows * n_cols - 1)
+    sums = remote(slots.at[others], slots.at[others], sum_send, sum_recv, at(1, 0))
     v3 = own(correlate((t2, t2_low), kt_high, kt_low, 96, 104), 96) + lv2
     for number, value in enumerate(p + powers(v1, v2, v3)):
         pixels[number] = swap_blocks(value)
-    for copy in first_copies:
-        copy.wait_recv()
-    meet(1)
-    total = first_slots[0]
-    for i in range(1, n_rows):
-        total = total + first_slots[i]
-    second_slots[col] = total
-    second_copies = gather(second_slots, col, n_cols, lambda d: at(0, d), second_send, second_recv)
-    for copy in second_copies:
-        copy.start()
-    for copy in second_copies:
-        copy.wait_recv()
-    total = second_slots[0]
-    for i in range(1, n_cols):
-        total = total + second_slots[i]
+    sums.wait_recv()
+    total = jnp.sum(slots[...], axis=0)
     total = jnp.sum(jnp.where(mine, jnp.broadcast_to(total, (8, 128)), 0.0), axis=1, keepdims=True)
     b0, c1, c2, c3, c4, c5 = [total[i : i + 1, :] for i in range(6)]
     c = (None, c1, c2, c3, c4, c5)
@@ -431,8 +425,9 @@
     template_ref[...] = guess_tile[...] + steps[0] * f2 + steps[1] * f1 + steps[2] * f0
     residual = r2[0] * f2 + r2[1] * f1 + r2[2] * f0
     residual_ref[...] = residual - alpha2 * (p2[0] * af2 + p2[1] * af1 + p2[2] * af0)
-    for copy in x_copies + b_copies + v_copies + first_copies + second_copies:
+    for copy in x_copies + b_copies + v_copies:
         copy.wait_send()
+    sums.wait_send()
 
 
 def on_device(grid, right_side, initial_guess, kernel):
@@ -465,9 +460,9 @@
             pltpu.VMEM((128, 128), F32), pltpu.VMEM((8, 96, 1024), BF16),
             weight, weight, weight, weight,
             tile, tile, tile, tile, tile, tile,
-            pltpu.VMEM((n_rows, 1, 128), F32), pltpu.VMEM((n_cols, 1, 128), F32), pltpu.VMEM((6, 64, LANES), F32), pltpu.SemaphoreType.REGULAR((2,)), tile, tile, pltpu.VMEM((31, 31), F32), dma((3,)),
+            pltpu.VMEM((n_rows * n_cols, 1, 128), F32), pltpu.VMEM((6, 64, LANES), F32), pltpu.SemaphoreType.REGULAR((3,)), tile, tile, pltpu.VMEM((31, 31), F32), dma((3,)),
             dma((8,)), dma((8,)), dma((8,)), dma((8,)), dma((8,)), dma((8,)),
-            dma((n_rows - 1,)), dma((n_rows - 1,)), dma((n_cols - 1,)), dma((n_cols - 1,)),
+            dma, dma,
         ],
         compiler_params=pltpu.CompilerParams(
             collective_id=0, has_side_effects=True, vmem_limit_bytes=16 * 1024 * 1024

time: 36.1 us -> 34 us (0.942)
  Pallas kernels: 33.9 us -> 32 us
    pallas_call x1, Pallas kernels: 33.9 us -> 32 us  [on_device(): pl.pallas_call(body, out_shape=(shape, shape), in_specs=[pl.BlockSpec(mem...]
where the time goes in v5:
time: 34 us; the launch traced here: 33.9 us
  Pallas kernels  32 us (94%)
  local copies, waits for them, and re-layouts  1.26 us (4%)
  between operations  0.64 us (2%)
    pallas_call x1, Pallas kernels, on_device(): pl.pallas_call(body, out_shape=(shape, shape), in_specs=[pl.BlockSpec(mem...  32 us
    unnamed x2, local copies, waits for them, and re-layouts  1.26 us

profile of v5, /device:TPU:1, one launch (start us, length us, event | category | flops | bytes accessed | tf_op | source)
XLA Modules:
  0.0 33.9 jit_solution(8191929091988503728)
XLA Ops:
  0.6 32.0 %shard_map.50 = (f32[64,256]{1,0:T(8,128)S(1)}, f32[64,256]{1,0:T(8,128)S(1)}) custom-call(f32[64,256]{1,0:T(8,128)} %refs_0_.1, f32[64,256]{1,0:T(8,128)} %refs_1_.1, f32[31,31]{1,0:T(8,128)} %refs_2_.1), custom_call_target="tpu_custom_call" | custom-call | tf_op jit(solution)/shard_map/pallas_call | solution.py:451
  32.6 0.6 %copy.7 = f32[64,256]{1,0:T(8,128)} copy(f32[64,256]{1,0:T(8,128)S(1)} %get-tuple-element.4) | data formatting | bytes 131072
  33.3 0.6 %copy.8 = f32[64,256]{1,0:T(8,128)} copy(f32[64,256]{1,0:T(8,128)S(1)} %get-tuple-element.5) | data formatting | bytes 131072

commit v6 on v5

--- a/solution.py
+++ b/solution.py
@@ -97,7 +97,12 @@
 SECOND_UNIT += [(1, -1, False), (-1, -1, True), (0, -1, True), (1, -1, True)]
 
 
-def correlate(field, high_weight, low_weight, first, count):
+def multiply(field, high_weight, low_weight, runs, finish):
+    count = sum(run[1] for run in runs)
+
+    def rows(part, di):
+        return jnp.concatenate([part[pl.ds(first + PITCH * di, length), :] for first, length in runs], axis=0)
+
     def body(middle, right, left0, left1):
         queues = []
         for unit, products in enumerate((FIRST_UNIT, SECOND_UNIT)):
@@ -112,15 +117,23 @@
                     weight = low_weight if low else high_weight
                     tile = weight[LANES * (di + 1) : LANES * (di + 2), LANES * (dj + 1) : LANES * (dj + 2)]
                     pltpu.matmul_push_rhs(tile, staging_register=register, mxu_index=unit)
-                    rows = pl.ds(first + PITCH * di, count)
-                    pltpu.matmul_acc_lhs(total, field[0][rows, :], load_staged_rhs=register)
+                    pltpu.matmul_acc_lhs(total, rows(field[0], di), load_staged_rhs=register)
                     if not low:
-                        pltpu.matmul_acc_lhs(total, field[1][rows, :])
-        value = pltpu.matmul_pop(middle) + roll(pltpu.matmul_pop(right), -1, 0)
-        return value + roll(pltpu.matmul_pop(left0) + pltpu.matmul_pop(left1), 1, 0)
+                        pltpu.matmul_acc_lhs(total, rows(field[1], di))
+        return finish(
+            pltpu.matmul_pop(middle), pltpu.matmul_pop(right), pltpu.matmul_pop(left0) + pltpu.matmul_pop(left1)
+        )
 
     totals = [pltpu.ACC(unit)((count, LANES), F32) for unit in (0, 1, 0, 1)]
     return pl.run_scoped(body, *totals)
+
+
+def combine(middle, right, left):
+    return middle + roll(right, -1, 0) + roll(left, 1, 0)
+
+
+def correlate(field, high_weight, low_weight, first, count):
+    return multiply(field, high_weight, low_weight, [(first, count)], combine)
 
 
 def smooth(source, first, count):
@@ -153,11 +166,16 @@
         right_ref[pair] = jnp.where(sublane < 4, roll(middle[first, 8:16], 4, 0), middle[second, 8:16])
 
 
-def unpack(middle, from_left, from_right, flat, masked):
+def unpack_middle(middle, flat, masked):
+    for r in range(12):
+        start = PITCH * r + 8
+        put(flat, start, masked(middle[r], start, 16))
+
+
+def unpack_sides(from_left, from_right, flat, masked):
     sublane = iota((8, LANES), 0)
     for r in range(ROWS):
-        right = jnp.zeros((8, LANES), F32)
-        left = right
+        right = left = jnp.zeros((8, LANES), F32)
         if r >= 1:
             right = from_right[(r - 1) // 2]
             if (r - 1) % 2:
@@ -166,19 +184,14 @@
             left = from_left[r // 2]
             if r % 2 == 0:
                 left = roll(left, 4, 0)
-        start = PITCH * r
-        put(flat, start, masked(jnp.where(sublane < 4, right, left), start, 8))
-        if r < 12:
-            put(flat, start + 8, masked(middle[r], start + 8, 16))
-        else:
-            put(flat, start + 8, jnp.zeros((16, LANES), F32))
+        put(flat, PITCH * r, masked(jnp.where(sublane < 4, right, left), PITCH * r, 8))
 
 
 def image_kernel(
     grid, b_ref, guess_ref, kernel_ref, template_ref, residual_ref,
     x_mid, v_mid, b_mid, x_left, x_right, v_left, v_right, b_left, b_right,
     x_from_left, x_from_right, v_from_left, v_from_right, b_from_left, b_from_right,
-    xf, xf_low, vf, vf_low, bf, rf, rf_low, t1, t1_low, t2, t2_low, mask_ref, taps_ref, shifted_ref, k_high, k_low, kt_high, kt_low,
+    xf, xf_low, vf, vf_low, bf, rf, rf_low, t1, t1_low, t2, t2_low, y_middle, y_right, y_left, mask_ref, taps_ref, shifted_ref, k_high, k_low, kt_high, kt_low,
     r0_own, v1_own, kr0_own, kv1_own, lr0_own, lv1_own,
     slots, pixels, far_sems, guess_tile, b_tile, taps_in, in_sems,
     x_send, x_recv, b_send, b_recv, v_send, v_recv, sum_send, sum_recv,
@@ -293,10 +306,34 @@
             if r < 10:
                 bf[PITCH * r + 8 : PITCH * r + 24] = b_mid[r - 2]
 
+    parts_refs = (y_middle, y_right, y_left)
+
+    def receive(copies, middle, from_left, from_right, field, greeting):
+        def keep(runs):
+            def finish(*parts):
+                for part, value in zip(parts_refs, parts):
+                    start = 0
+                    for first, length in runs:
+                        part[pl.ds(first, length), :] = value[start : start + length]
+                        start += length
+
+            return finish
+
+        for copy in copies[6:]:
+            copy.wait_recv()
+        unpack_middle(middle, field, masked)
+        runs = [(PITCH * r + 8, 16) for r in range(1, 11)]
+        multiply(field, k_high, k_low, runs, keep(runs))
+        for copy in copies[:6]:
+            copy.wait_recv()
+        greeting()
+        unpack_sides(from_left, from_right, field, masked)
+        runs = [(PITCH * r, 8) for r in range(1, 12)]
+        multiply(field, k_high, k_low, runs, keep(runs))
+        value = combine(*[part[pl.ds(24, 248), :] for part in parts_refs])
+        put((t1, t1_low), 24, masked(value, 24, 248))
+
     def apply_twice(source, second, between):
-        for first, count, keep, kept in ((24, 152, 24, 144), (160, 112, 168, 104)):
-            value = correlate(source, k_high, k_low, first, count)[keep - first : keep - first + kept]
-            put((t1, t1_low), keep, masked(value, keep, kept))
         between()
         smooth_source = []
         for first, count, keep, kept in ((48, 104, 48, 96), (136, 112, 144, 104)):
@@ -314,10 +351,7 @@
             own(smooth(second[0], 96, 104), 96),
         )
 
-    for copy in x_copies:
-        copy.wait_recv()
-    greet(0)
-    unpack(x_mid, x_from_left, x_from_right, (xf, xf_low), masked)
+    receive(x_copies, x_mid, x_from_left, x_from_right, (xf, xf_low), lambda: greet(0))
     _, _, kr0, lr0 = apply_twice((xf, xf_low), (rf, rf_low), take_b)
     v1 = own(correlate((t2, t2_low), kt_high, kt_low, 96, 104), 96) + lr0
     spread(v_mid, 4, v1)
@@ -332,11 +366,11 @@
     kr0_own[...] = kr0
     lr0_own[...] = lr0
 
-    for copy in v_copies:
-        copy.wait_recv()
-    meet(1)
-    greet(2)
-    unpack(v_mid, v_from_left, v_from_right, (vf, vf_low), masked)
+    def meet_and_greet():
+        meet(1)
+        greet(2)
+
+    receive(v_copies, v_mid, v_from_left, v_from_right, (vf, vf_low), meet_and_greet)
     kv1, lv1, kv2, lv2 = apply_twice((vf, vf_low), (rf, rf_low), lambda: None)
     v2 = own(rf[pl.ds(96, 104), :], 96)
 
@@ -448,7 +482,7 @@
     def body(*refs):
         image_kernel(grid, *refs)
 
-    return pl.pallas_call(
+    results = pl.pallas_call(
         body,
         out_shape=(shape, shape),
         in_specs=[pl.BlockSpec(memory_space=pltpu.HBM)] * 3,
@@ -456,7 +490,7 @@
         scratch_shapes=[
             middle, middle, b_middle, side, side, side, side, b_side, b_side,
             halo, halo, halo, halo, b_halo, b_halo,
-            flat, flat, flat, flat, flat, flat, flat, flat, flat, flat, flat, flat,
+            flat, flat, flat, flat, flat, flat, flat, flat, flat, flat, flat, flat, flat, flat, flat,
             pltpu.VMEM((128, 128), F32), pltpu.VMEM((8, 96, 1024), BF16),
             weight, weight, weight, weight,
             tile, tile, tile, tile, tile, tile,
@@ -469,6 +503,25 @@
         ),
     )(*(pltpu.with_memory_space_constraint(x, pltpu.HBM) for x in (right_side, initial_guess, kernel)))
 
+    def store(template_ref, residual_ref, template_out, residual_out, sems):
+        copies = (
+            pltpu.make_async_copy(template_ref, template_out, sems.at[0]),
+            pltpu.make_async_copy(residual_ref, residual_out, sems.at[1]),
+        )
+        for copy in copies:
+            copy.start()
+        for copy in copies:
+            copy.wait()
+
+    return pl.pallas_call(
+        store,
+        out_shape=(shape, shape),
+        in_specs=[vmem] * 2,
+        out_specs=(pl.BlockSpec(memory_space=pltpu.HBM),) * 2,
+        scratch_shapes=[dma((2,))],
+        compiler_params=pltpu.CompilerParams(vmem_limit_bytes=1024 * 1024),
+    )(*results)
+
 
 def solution(mesh):
     grid = (mesh.shape["row"], mesh.shape["col"])

time: 34 us -> 32.6 us (0.959)
  local copies, waits for them, and re-layouts: 1.26 us -> 0 us
    unnamed x2 -> x0, local copies, waits for them, and re-layouts: 1.26 us -> none
    pallas_call x1, Pallas kernels: 32 us -> 31.2 us  [on_device(): pl.pallas_call(body, out_shape=(shape, shape), in_specs=[pl.BlockSpec(mem...]
    pallas_call x0 -> x1, Pallas kernels: none -> 0.67 us  [on_device(): pl.pallas_call(store, out_shape=(shape, shape), in_specs=[vmem] * 2, out_...]
where the time goes in v6:
time: 32.6 us; the launch traced here: 32.5 us
  Pallas kernels  31.8 us (98%)
  between operations  0.64 us (2%)
    pallas_call x1, Pallas kernels, on_device(): pl.pallas_call(body, out_shape=(shape, shape), in_specs=[pl.BlockSpec(mem...  31.2 us
    pallas_call x1, Pallas kernels, on_device(): pl.pallas_call(store, out_shape=(shape, shape), in_specs=[vmem] * 2, out_...  0.67 us

profile of v6, /device:TPU:1, one launch (start us, length us, event | category | flops | bytes accessed | tf_op | source)
XLA Modules:
  0.0 32.5 jit_solution(17994059736010442868)
XLA Ops:
  0.6 31.2 %shard_map.50 = (f32[64,256]{1,0:T(8,128)S(1)}, f32[64,256]{1,0:T(8,128)S(1)}) custom-call(f32[64,256]{1,0:T(8,128)} %refs_0_.1, f32[64,256]{1,0:T(8,128)} %refs_1_.1, f32[31,31]{1,0:T(8,128)} %refs_2_.1), custom_call_target="tpu_custom_call" | custom-call | tf_op jit(solution)/shard_map/pallas_call | solution.py:485
  31.8 0.7 %shard_map.51 = (f32[64,256]{1,0:T(8,128)}, f32[64,256]{1,0:T(8,128)}) custom-call(f32[64,256]{1,0:T(8,128)S(1)} %get-tuple-element.4.template_ref, f32[64,256]{1,0:T(8,128)S(1)} %get-tuple-element.5.residual_ref), custom_call_target="tpu_custom_call" | custom-call | tf_op jit(solution)/shard_map/pallas_call | solution.py:516

commit v7 on v6

--- a/solution.py
+++ b/solution.py
@@ -308,7 +308,7 @@
 
     parts_refs = (y_middle, y_right, y_left)
 
-    def receive(copies, middle, from_left, from_right, field, greeting):
+    def receive(copies, middle, from_left, from_right, field, greeting, top, bottom):
         def keep(runs):
             def finish(*parts):
                 for part, value in zip(parts_refs, parts):
@@ -322,37 +322,43 @@
         for copy in copies[6:]:
             copy.wait_recv()
         unpack_middle(middle, field, masked)
-        runs = [(PITCH * r + 8, 16) for r in range(1, 11)]
+        runs = [(PITCH * r + 8, 16) for r in range(top, bottom)]
         multiply(field, k_high, k_low, runs, keep(runs))
         for copy in copies[:6]:
             copy.wait_recv()
         greeting()
         unpack_sides(from_left, from_right, field, masked)
-        runs = [(PITCH * r, 8) for r in range(1, 12)]
+        runs = [(PITCH * r, 8) for r in range(top, bottom + 1)]
         multiply(field, k_high, k_low, runs, keep(runs))
-        value = combine(*[part[pl.ds(24, 248), :] for part in parts_refs])
-        put((t1, t1_low), 24, masked(value, 24, 248))
-
-    def apply_twice(source, second, between):
-        between()
-        smooth_source = []
-        for first, count, keep, kept in ((48, 104, 48, 96), (136, 112, 144, 104)):
-            value = correlate((t1, t1_low), kt_high, kt_low, first, count)[keep - first : keep - first + kept]
-            smooth_source.append(smooth(source[0], keep, kept))
-            value = value + smooth_source[-1]
-            put(second, keep, masked(bf[pl.ds(keep, kept), :] - value if source[0] is xf else value, keep, kept))
-        for first, count, keep, kept in ((72, 56, 72, 48), (112, 112, 120, 104)):
-            value = correlate(second, k_high, k_low, first, count)[keep - first : keep - first + kept]
-            put((t2, t2_low), keep, masked(value, keep, kept))
-        return (
-            own(t1[pl.ds(96, 104), :], 96),
-            own(jnp.concatenate(smooth_source, axis=0), 48),
-            own(t2[pl.ds(96, 104), :], 96),
-            own(smooth(second[0], 96, 104), 96),
-        )
-
-    receive(x_copies, x_mid, x_from_left, x_from_right, (xf, xf_low), lambda: greet(0))
-    _, _, kr0, lr0 = apply_twice((xf, xf_low), (rf, rf_low), take_b)
+        first, count = PITCH * top, PITCH * (bottom - top) + 8
+        value = combine(*[part[pl.ds(first, count), :] for part in parts_refs])
+        put((t1, t1_low), first, masked(value, first, count))
+
+    blur, blur_back = (k_high, k_low), (kt_high, kt_low)
+    blurred, second, blurred_second = (t1, t1_low), (rf, rf_low), (t2, t2_low)
+
+    def stage(source, weights, target, runs, extra=None):
+        value = multiply(source, *weights, [run[:2] for run in runs], combine)
+        start = 0
+        for first, count, keep, kept in runs:
+            piece = value[start + keep - first : start + keep - first + kept]
+            start += count
+            if extra is not None:
+                piece = extra(piece, keep, kept)
+            put(target, keep, masked(piece, keep, kept))
+
+    receive(x_copies, x_mid, x_from_left, x_from_right, (xf, xf_low), lambda: greet(0), 1, 11)
+    take_b()
+
+    def remainder(piece, keep, kept):
+        return bf[pl.ds(keep, kept), :] - (piece + smooth(xf, keep, kept))
+
+    stage(blurred, blur_back, second, [(48, 136, 48, 128)], remainder)
+    stage(blurred, blur_back, second, [(168, 80, 176, 72)], remainder)
+    stage(second, blur, blurred_second, [(72, 80, 72, 72)])
+    stage(second, blur, blurred_second, [(136, 88, 144, 80)])
+    kr0 = own(t2[pl.ds(96, 104), :], 96)
+    lr0 = own(smooth(rf, 96, 104), 96)
     v1 = own(correlate((t2, t2_low), kt_high, kt_low, 96, 104), 96) + lr0
     spread(v_mid, 4, v1)
     pack_sides(v_mid, v_left, v_right)
@@ -370,8 +376,18 @@
         meet(1)
         greet(2)
 
-    receive(v_copies, v_mid, v_from_left, v_from_right, (vf, vf_low), meet_and_greet)
-    kv1, lv1, kv2, lv2 = apply_twice((vf, vf_low), (rf, rf_low), lambda: None)
+    receive(v_copies, v_mid, v_from_left, v_from_right, (vf, vf_low), meet_and_greet, 2, 10)
+    smooth_pieces = []
+
+    def image(piece, keep, kept):
+        smooth_pieces.append(smooth(vf, keep, kept))
+        return piece + smooth_pieces[-1]
+
+    stage(blurred, blur_back, second, [(64, 88, 72, 72)], image)
+    stage(blurred, blur_back, second, [(136, 96, 144, 80)], image)
+    stage(second, blur, blurred_second, [(96, 104, 104, 88)])
+    kv1, kv2 = own(t1[pl.ds(96, 104), :], 96), own(t2[pl.ds(96, 104), :], 96)
+    lv1, lv2 = own(jnp.concatenate(smooth_pieces, axis=0), 72), own(smooth(rf, 96, 104), 96)
     v2 = own(rf[pl.ds(96, 104), :], 96)
 
     def powers(zero, one, two):
@@ -415,6 +431,11 @@
         remote(slots.at[me], slots.at[me], sum_send, sum_recv, (rows_at[dr], cols_at[dc])).start()
     others = pl.ds(0, n_rows * n_cols - 1)
     sums = remote(slots.at[others], slots.at[others], sum_send, sum_recv, at(1, 0))
+    for copy in x_copies + b_copies + v_copies:
+        copy.wait_send()
+    stage((vf, vf_low), blur, blurred, [(24, 40, 24, 32), (232, 40, 240, 32)])
+    stage(blurred, blur_back, second, [(48, 40, 48, 32), (208, 40, 216, 32)], image)
+    stage(second, blur, blurred_second, [(72, 40, 72, 32), (184, 40, 192, 32)])
     v3 = own(correlate((t2, t2_low), kt_high, kt_low, 96, 104), 96) + lv2
     for number, value in enumerate(p + powers(v1, v2, v3)):
         pixels[number] = swap_blocks(value)
@@ -459,8 +480,6 @@
     template_ref[...] = guess_tile[...] + steps[0] * f2 + steps[1] * f1 + steps[2] * f0
     residual = r2[0] * f2 + r2[1] * f1 + r2[2] * f0
     residual_ref[...] = residual - alpha2 * (p2[0] * af2 + p2[1] * af1 + p2[2] * af0)
-    for copy in x_copies + b_copies + v_copies:
-        copy.wait_send()
     sums.wait_send()
 
 

time: 32.6 us -> 31.6 us (0.969)
  Pallas kernels: 31.8 us -> 30.8 us
    pallas_call x1, Pallas kernels: 31.2 us -> 30.1 us  [on_device(): pl.pallas_call(body, out_shape=(shape, shape), in_specs=[pl.BlockSpec(mem...]
where the time goes in v7:
time: 31.6 us; the launch traced here: 31.5 us
  Pallas kernels  30.8 us (97%)
  between operations  0.64 us (2%)
    pallas_call x1, Pallas kernels, on_device(): pl.pallas_call(body, out_shape=(shape, shape), in_specs=[pl.BlockSpec(mem...  30.1 us
    pallas_call x1, Pallas kernels, on_device(): pl.pallas_call(store, out_shape=(shape, shape), in_specs=[vmem] * 2, out_...  0.67 us

profile of v7, /device:TPU:1, one launch (start us, length us, event | category | flops | bytes accessed | tf_op | source)
XLA Modules:
  0.0 31.5 jit_solution(596749605774061265)
XLA Ops:
  0.6 30.1 %shard_map.50 = (f32[64,256]{1,0:T(8,128)S(1)}, f32[64,256]{1,0:T(8,128)S(1)}) custom-call(f32[64,256]{1,0:T(8,128)} %refs_0_.1, f32[64,256]{1,0:T(8,128)} %refs_1_.1, f32[31,31]{1,0:T(8,128)} %refs_2_.1), custom_call_target="tpu_custom_call" | custom-call | tf_op jit(solution)/shard_map/pallas_call | solution.py:504
  30.8 0.7 %shard_map.51 = (f32[64,256]{1,0:T(8,128)}, f32[64,256]{1,0:T(8,128)}) custom-call(f32[64,256]{1,0:T(8,128)S(1)} %get-tuple-element.4.template_ref, f32[64,256]{1,0:T(8,128)S(1)} %get-tuple-element.5.residual_ref), custom_call_target="tpu_custom_call" | custom-call | tf_op jit(solution)/shard_map/pallas_call | solution.py:535

commit v8 on v7

--- a/solution.py
+++ b/solution.py
@@ -210,14 +210,40 @@
     for load in loads:
         load.start()
     barrier = pltpu.get_barrier_semaphore()
-    partners = [at(dr, dc) for dr, dc in DIRECTIONS[:6]] + [at(d, 0) for d in range(1, n_rows)]
-    for partner in partners:
-        pl.semaphore_signal(barrier, inc=1, device_id=partner, device_id_type=MESH)
+    def signal(semaphore, device):
+        pl.semaphore_signal(semaphore, inc=1, device_id=device, device_id_type=MESH)
+
+    def exists(dr, dc):
+        inside = None
+        for place, step, count in ((row, dr, n_rows), (col, dc, n_cols)):
+            if step:
+                test = place + step < count if step > 0 else place + step >= 0
+                inside = test if inside is None else inside & test
+        return inside
+
+    for dr, dc in DIRECTIONS[:6]:
+        pl.when(exists(dr, dc))(lambda dr=dr, dc=dc: signal(barrier, at(dr, dc)))
+    for d in range(1, n_rows):
+        signal(barrier, at(d, 0))
+    greetings = n_rows - 1 + sum(exists(dr, dc).astype(jnp.int32) for dr, dc in DIRECTIONS[:6])
 
     def remote(source, target, send, recv, device):
         return pltpu.make_async_remote_copy(
             src_ref=source, dst_ref=target, send_sem=send, recv_sem=recv, device_id=device, device_id_type=MESH
         )
+
+    def start(copies):
+        for (dr, dc), copy in zip(DIRECTIONS, copies):
+            pl.when(exists(dr, dc))(copy.start)
+
+    def sent(copies):
+        for (dr, dc), copy in zip(DIRECTIONS, copies):
+            pl.when(exists(dr, dc))(copy.wait_send)
+
+    def received(copies, numbers=range(8)):
+        for number in numbers:
+            dr, dc = DIRECTIONS[number]
+            pl.when(exists(-dr, -dc))(copies[number].wait_recv)
 
     def field_copies(middle, left, right, from_left, from_right, send, recv):
         copies = []
@@ -238,11 +264,10 @@
     loads[0].wait()
     spread(x_mid, 4, swap_blocks(guess_tile[...]))
     pack_sides(x_mid, x_left, x_right)
-    pl.semaphore_wait(barrier, n_rows - 1 + 6)
+    pl.semaphore_wait(barrier, greetings)
 
     x_copies = field_copies(x_mid, x_left, x_right, x_from_left, x_from_right, x_send, x_recv)
-    for copy in x_copies:
-        copy.start()
+    start(x_copies)
     loads[1].wait()
     spread(b_mid, 2, swap_blocks(b_tile[...]))
     sublane = iota((8, LANES), 0)
@@ -263,8 +288,7 @@
             source = b_right if dc == 1 else b_left
             target = (b_from_left if dc == 1 else b_from_right).at[1 - dr]
         b_copies.append(remote(source, target, b_send.at[number], b_recv.at[number], at(dr, dc)))
-    for copy in b_copies:
-        copy.start()
+    start(b_copies)
 
     taps_ref[...] = jnp.zeros_like(taps_ref)
     loads[2].wait()
@@ -281,21 +305,22 @@
         return jnp.where(mask_ref[pl.ds(first, count), :] > 0.5, value, 0.0)
 
     distances = []
-    while 2 << len(distances) <= n_cols // 2:
+    while (2 << len(distances)) - 1 < n_cols - 1:
         distances.append(2 << len(distances))
 
     def greet(number):
         if number < len(distances):
-            for d in sorted({distances[number], n_cols - distances[number]}):
-                pl.semaphore_signal(far_sems.at[number], inc=1, device_id=at(0, d), device_id_type=MESH)
+            for d in (distances[number], -distances[number]):
+                pl.when(exists(0, d))(lambda d=d: signal(far_sems.at[number], at(0, d)))
 
     def meet(number):
         if number < len(distances):
-            pl.semaphore_wait(far_sems.at[number], 1 if 2 * distances[number] == n_cols else 2)
+            d = distances[number]
+            count = exists(0, d).astype(jnp.int32) + exists(0, -d).astype(jnp.int32)
+            pl.semaphore_wait(far_sems.at[number], count)
 
     def take_b():
-        for copy in b_copies:
-            copy.wait_recv()
+        received(b_copies)
         for r in range(2, 11):
             right = left = jnp.zeros((8, LANES), F32)
             if r >= 3:
@@ -319,13 +344,11 @@
 
             return finish
 
-        for copy in copies[6:]:
-            copy.wait_recv()
+        received(copies, range(6, 8))
         unpack_middle(middle, field, masked)
         runs = [(PITCH * r + 8, 16) for r in range(top, bottom)]
         multiply(field, k_high, k_low, runs, keep(runs))
-        for copy in copies[:6]:
-            copy.wait_recv()
+        received(copies, range(6))
         greeting()
         unpack_sides(from_left, from_right, field, masked)
         runs = [(PITCH * r, 8) for r in range(top, bottom + 1)]
@@ -363,8 +386,7 @@
     spread(v_mid, 4, v1)
     pack_sides(v_mid, v_left, v_right)
     v_copies = field_copies(v_mid, v_left, v_right, v_from_left, v_from_right, v_send, v_recv)
-    for copy in v_copies:
-        copy.start()
+    start(v_copies)
     meet(0)
     greet(1)
     r0_own[...] = own(rf[pl.ds(96, 104), :], 96)
@@ -431,8 +453,8 @@
         remote(slots.at[me], slots.at[me], sum_send, sum_recv, (rows_at[dr], cols_at[dc])).start()
     others = pl.ds(0, n_rows * n_cols - 1)
     sums = remote(slots.at[others], slots.at[others], sum_send, sum_recv, at(1, 0))
-    for copy in x_copies + b_copies + v_copies:
-        copy.wait_send()
+    for copies in (x_copies, b_copies, v_copies):
+        sent(copies)
     stage((vf, vf_low), blur, blurred, [(24, 40, 24, 32), (232, 40, 240, 32)])
     stage(blurred, blur_back, second, [(48, 40, 48, 32), (208, 40, 216, 32)], image)
     stage(second, blur, blurred_second, [(72, 40, 72, 32), (184, 40, 192, 32)])
@@ -440,7 +462,10 @@
     for number, value in enumerate(p + powers(v1, v2, v3)):
         pixels[number] = swap_blocks(value)
     sums.wait_recv()
-    total = jnp.sum(slots[...], axis=0)
+    groups = [jnp.sum(slots[pl.ds(start, n_cols)], axis=0) for start in range(0, n_rows * n_cols, n_cols)]
+    while len(groups) > 1:
+        groups = [sum(groups[i : i + 2][1:], groups[i]) for i in range(0, len(groups), 2)]
+    total = groups[0]
     total = jnp.sum(jnp.where(mine, jnp.broadcast_to(total, (8, 128)), 0.0), axis=1, keepdims=True)
     b0, c1, c2, c3, c4, c5 = [total[i : i + 1, :] for i in range(6)]
     c = (None, c1, c2, c3, c4, c5)

time: 31.6 us -> 29.6 us (0.937)
  Pallas kernels: 30.8 us -> 28.8 us
    pallas_call x1, Pallas kernels: 30.1 us -> 28.1 us  [on_device(): pl.pallas_call(body, out_shape=(shape, shape), in_specs=[pl.BlockSpec(mem...]
where the time goes in v8:
time: 29.6 us; the launch traced here: 29.4 us
  Pallas kernels  28.8 us (97%)
  between operations  0.64 us (2%)
    pallas_call x1, Pallas kernels, on_device(): pl.pallas_call(body, out_shape=(shape, shape), in_specs=[pl.BlockSpec(mem...  28.1 us
    pallas_call x1, Pallas kernels, on_device(): pl.pallas_call(store, out_shape=(shape, shape), in_specs=[vmem] * 2, out_...  0.67 us

profile of v8, /device:TPU:1, one launch (start us, length us, event | category | flops | bytes accessed | tf_op | source)
XLA Modules:
  0.0 29.4 jit_solution(5943733806044846751)
XLA Ops:
  0.6 28.1 %shard_map.50 = (f32[64,256]{1,0:T(8,128)S(1)}, f32[64,256]{1,0:T(8,128)S(1)}) custom-call(f32[64,256]{1,0:T(8,128)} %refs_0_.1, f32[64,256]{1,0:T(8,128)} %refs_1_.1, f32[31,31]{1,0:T(8,128)} %refs_2_.1), custom_call_target="tpu_custom_call" | custom-call | tf_op jit(solution)/shard_map/pallas_call | solution.py:529
  28.8 0.7 %shard_map.51 = (f32[64,256]{1,0:T(8,128)}, f32[64,256]{1,0:T(8,128)}) custom-call(f32[64,256]{1,0:T(8,128)S(1)} %get-tuple-element.4.template_ref, f32[64,256]{1,0:T(8,128)S(1)} %get-tuple-element.5.residual_ref), custom_call_target="tpu_custom_call" | custom-call | tf_op jit(solution)/shard_map/pallas_call | solution.py:560

commit v9 on v8

--- a/solution.py
+++ b/solution.py
@@ -92,9 +92,10 @@
                         ] = shifted_ref[start % 8, rows : rows + 16, lanes : lanes + LANES]
 
 
-FIRST_UNIT = [(di, 0, low) for low in (False, True) for di in (-1, 0, 1)] + [(-1, -1, False), (0, -1, False)]
+FIRST_UNIT = [(di, 0, low) for low in (False, True) for di in (-1, 0, 1)]
+FIRST_UNIT += [(-1, -1, False), (-1, -1, True), (0, -1, True)]
 SECOND_UNIT = [(di, 1, low) for low in (False, True) for di in (-1, 0, 1)]
-SECOND_UNIT += [(1, -1, False), (-1, -1, True), (0, -1, True), (1, -1, True)]
+SECOND_UNIT += [(0, -1, False), (1, -1, False), (1, -1, True)]
 
 
 def multiply(field, high_weight, low_weight, runs, finish):
@@ -360,26 +361,25 @@
     blur, blur_back = (k_high, k_low), (kt_high, kt_low)
     blurred, second, blurred_second = (t1, t1_low), (rf, rf_low), (t2, t2_low)
 
-    def stage(source, weights, target, runs, extra=None):
+    def stage(source, weights, target, runs, term=None, sign=1.0):
+        terms = [None if term is None else term(keep, kept) for first, count, keep, kept in runs]
         value = multiply(source, *weights, [run[:2] for run in runs], combine)
         start = 0
-        for first, count, keep, kept in runs:
+        for (first, count, keep, kept), added in zip(runs, terms):
             piece = value[start + keep - first : start + keep - first + kept]
             start += count
-            if extra is not None:
-                piece = extra(piece, keep, kept)
+            if added is not None:
+                piece = added + sign * piece
             put(target, keep, masked(piece, keep, kept))
 
     receive(x_copies, x_mid, x_from_left, x_from_right, (xf, xf_low), lambda: greet(0), 1, 11)
     take_b()
 
-    def remainder(piece, keep, kept):
-        return bf[pl.ds(keep, kept), :] - (piece + smooth(xf, keep, kept))
-
-    stage(blurred, blur_back, second, [(48, 136, 48, 128)], remainder)
-    stage(blurred, blur_back, second, [(168, 80, 176, 72)], remainder)
-    stage(second, blur, blurred_second, [(72, 80, 72, 72)])
-    stage(second, blur, blurred_second, [(136, 88, 144, 80)])
+    def remainder(keep, kept):
+        return bf[pl.ds(keep, kept), :] - smooth(xf, keep, kept)
+
+    stage(blurred, blur_back, second, [(48, 200, 48, 200)], remainder, -1.0)
+    stage(second, blur, blurred_second, [(72, 152, 72, 152)])
     kr0 = own(t2[pl.ds(96, 104), :], 96)
     lr0 = own(smooth(rf, 96, 104), 96)
     v1 = own(correlate((t2, t2_low), kt_high, kt_low, 96, 104), 96) + lr0
@@ -401,12 +401,11 @@
     receive(v_copies, v_mid, v_from_left, v_from_right, (vf, vf_low), meet_and_greet, 2, 10)
     smooth_pieces = []
 
-    def image(piece, keep, kept):
+    def image(keep, kept):
         smooth_pieces.append(smooth(vf, keep, kept))
-        return piece + smooth_pieces[-1]
-
-    stage(blurred, blur_back, second, [(64, 88, 72, 72)], image)
-    stage(blurred, blur_back, second, [(136, 96, 144, 80)], image)
+        return smooth_pieces[-1]
+
+    stage(blurred, blur_back, second, [(72, 152, 72, 152)], image)
     stage(second, blur, blurred_second, [(96, 104, 104, 88)])
     kv1, kv2 = own(t1[pl.ds(96, 104), :], 96), own(t2[pl.ds(96, 104), :], 96)
     lv1, lv2 = own(jnp.concatenate(smooth_pieces, axis=0), 72), own(smooth(rf, 96, 104), 96)

time: 29.6 us -> 29.3 us (0.990)
  Pallas kernels: 28.8 us -> 28.5 us
    pallas_call x1, Pallas kernels: 28.1 us -> 27.8 us  [on_device(): pl.pallas_call(body, out_shape=(shape, shape), in_specs=[pl.BlockSpec(mem...]
where the time goes in v9:
time: 29.3 us; the launch traced here: 29.1 us
  Pallas kernels  28.5 us (97%)
  between operations  0.64 us (2%)
    pallas_call x1, Pallas kernels, on_device(): pl.pallas_call(body, out_shape=(shape, shape), in_specs=[pl.BlockSpec(mem...  27.8 us
    pallas_call x1, Pallas kernels, on_device(): pl.pallas_call(store, out_shape=(shape, shape), in_specs=[vmem] * 2, out_...  0.67 us

profile of v9, /device:TPU:1, one launch (start us, length us, event | category | flops | bytes accessed | tf_op | source)
XLA Modules:
  0.0 29.1 jit_solution(3437531121960865592)
XLA Ops:
  0.6 27.8 %shard_map.50 = (f32[64,256]{1,0:T(8,128)S(1)}, f32[64,256]{1,0:T(8,128)S(1)}) custom-call(f32[64,256]{1,0:T(8,128)} %refs_0_.1, f32[64,256]{1,0:T(8,128)} %refs_1_.1, f32[31,31]{1,0:T(8,128)} %refs_2_.1), custom_call_target="tpu_custom_call" | custom-call | tf_op jit(solution)/shard_map/pallas_call | solution.py:528
  28.4 0.7 %shard_map.51 = (f32[64,256]{1,0:T(8,128)}, f32[64,256]{1,0:T(8,128)}) custom-call(f32[64,256]{1,0:T(8,128)S(1)} %get-tuple-element.4.template_ref, f32[64,256]{1,0:T(8,128)S(1)} %get-tuple-element.5.residual_ref), custom_call_target="tpu_custom_call" | custom-call | tf_op jit(solution)/shard_map/pallas_call | solution.py:559

commit v10 on v9

--- a/solution.py
+++ b/solution.py
@@ -31,7 +31,9 @@
 def put(pair, first, value):
     rows = pl.ds(first, value.shape[0])
     pair[0][rows, :] = value
-    pair[1][rows, :] = value - rounded(value)
+    rest = value - rounded(value)
+    pair[1][rows, :] = rest
+    pair[2][rows, :] = rest - rounded(rest)
 
 
 def swap_blocks(x):
@@ -77,9 +79,11 @@
             moved = roll(base, -B * shift, 1)
             high = moved.astype(BF16)
             shifted_ref[shift, 0:48] = high
-            shifted_ref[shift, 48:96] = (moved - high.astype(F32)).astype(BF16)
-        for part in range(2):
-            weight = weights[2 * number + part]
+            rest = moved - high.astype(F32)
+            shifted_ref[shift, 48:96] = rest.astype(BF16)
+            shifted_ref[shift, 96:144] = (rest - rounded(rest)).astype(BF16)
+        for part in range(3):
+            weight = weights[number][part]
             for di in (-1, 0, 1):
                 for r in range(B):
                     start = 31 - 16 * di - r
@@ -92,13 +96,13 @@
                         ] = shifted_ref[start % 8, rows : rows + 16, lanes : lanes + LANES]
 
 
-FIRST_UNIT = [(di, 0, low) for low in (False, True) for di in (-1, 0, 1)]
-FIRST_UNIT += [(-1, -1, False), (-1, -1, True), (0, -1, True)]
-SECOND_UNIT = [(di, 1, low) for low in (False, True) for di in (-1, 0, 1)]
-SECOND_UNIT += [(0, -1, False), (1, -1, False), (1, -1, True)]
-
-
-def multiply(field, high_weight, low_weight, runs, finish):
+FIRST_UNIT = [(di, 0, part) for part in range(3) for di in (-1, 0, 1)]
+FIRST_UNIT += [(-1, -1, 0), (0, -1, 0), (-1, -1, 2), (0, -1, 2), (1, -1, 2)]
+SECOND_UNIT = [(di, 1, part) for part in range(3) for di in (-1, 0, 1)]
+SECOND_UNIT += [(1, -1, 0), (-1, -1, 1), (0, -1, 1), (1, -1, 1)]
+
+
+def multiply(field, weights, runs, finish):
     count = sum(run[1] for run in runs)
 
     def rows(part, di):
@@ -108,19 +112,19 @@
         queues = []
         for unit, products in enumerate((FIRST_UNIT, SECOND_UNIT)):
             queue = []
-            for number, (di, dj, low) in enumerate(products):
-                queue.append((unit, number % 2, di, dj, low, ((left0, left1)[unit], middle, right)[dj + 1]))
+            for number, (di, dj, part) in enumerate(products):
+                queue.append((unit, number % 2, di, dj, part, ((left0, left1)[unit], middle, right)[dj + 1]))
             queues.append(queue)
         for step in range(max(map(len, queues))):
             for queue in queues:
                 if step < len(queue):
-                    unit, register, di, dj, low, total = queue[step]
-                    weight = low_weight if low else high_weight
+                    unit, register, di, dj, part, total = queue[step]
+                    weight = weights[part]
                     tile = weight[LANES * (di + 1) : LANES * (di + 2), LANES * (dj + 1) : LANES * (dj + 2)]
                     pltpu.matmul_push_rhs(tile, staging_register=register, mxu_index=unit)
                     pltpu.matmul_acc_lhs(total, rows(field[0], di), load_staged_rhs=register)
-                    if not low:
-                        pltpu.matmul_acc_lhs(total, rows(field[1], di))
+                    for other in range(1, 3 - part):
+                        pltpu.matmul_acc_lhs(total, rows(field[other], di))
         return finish(
             pltpu.matmul_pop(middle), pltpu.matmul_pop(right), pltpu.matmul_pop(left0) + pltpu.matmul_pop(left1)
         )
@@ -133,8 +137,8 @@
     return middle + roll(right, -1, 0) + roll(left, 1, 0)
 
 
-def correlate(field, high_weight, low_weight, first, count):
-    return multiply(field, high_weight, low_weight, [(first, count)], combine)
+def correlate(field, weights, first, count):
+    return multiply(field, weights, [(first, count)], combine)
 
 
 def smooth(source, first, count):
@@ -192,7 +196,7 @@
     grid, b_ref, guess_ref, kernel_ref, template_ref, residual_ref,
     x_mid, v_mid, b_mid, x_left, x_right, v_left, v_right, b_left, b_right,
     x_from_left, x_from_right, v_from_left, v_from_right, b_from_left, b_from_right,
-    xf, xf_low, vf, vf_low, bf, rf, rf_low, t1, t1_low, t2, t2_low, y_middle, y_right, y_left, mask_ref, taps_ref, shifted_ref, k_high, k_low, kt_high, kt_low,
+    xf, xf_low, xf_last, vf, vf_low, vf_last, bf, rf, rf_low, rf_last, t1, t1_low, t1_last, t2, t2_low, t2_last, y_middle, y_right, y_left, mask_ref, taps_ref, shifted_ref, k_high, k_low, k_last, kt_high, kt_low, kt_last,
     r0_own, v1_own, kr0_own, kv1_own, lr0_own, lv1_own,
     slots, pixels, far_sems, guess_tile, b_tile, taps_in, in_sems,
     x_send, x_recv, b_send, b_recv, v_send, v_recv, sum_send, sum_recv,
@@ -292,9 +296,11 @@
     start(b_copies)
 
     taps_ref[...] = jnp.zeros_like(taps_ref)
+    blur, blur_back = (k_high, k_low, k_last), (kt_high, kt_low, kt_last)
+    blurred, second, blurred_second = (t1, t1_low, t1_last), (rf, rf_low, rf_last), (t2, t2_low, t2_last)
     loads[2].wait()
     taps_ref[0:31, 0:31] = taps_in[...]
-    build_weights(taps_ref, shifted_ref, (k_high, k_low, kt_high, kt_low))
+    build_weights(taps_ref, shifted_ref, (blur, blur_back))
     flat = iota((FLAT, LANES), 0)
     slot = flat % PITCH
     block_row = row * 4 + flat // PITCH - 4 - (slot < 4).astype(jnp.int32)
@@ -348,22 +354,20 @@
         received(copies, range(6, 8))
         unpack_middle(middle, field, masked)
         runs = [(PITCH * r + 8, 16) for r in range(top, bottom)]
-        multiply(field, k_high, k_low, runs, keep(runs))
+        multiply(field, blur, runs, keep(runs))
         received(copies, range(6))
         greeting()
         unpack_sides(from_left, from_right, field, masked)
         runs = [(PITCH * r, 8) for r in range(top, bottom + 1)]
-        multiply(field, k_high, k_low, runs, keep(runs))
+        multiply(field, blur, runs, keep(runs))
         first, count = PITCH * top, PITCH * (bottom - top) + 8
         value = combine(*[part[pl.ds(first, count), :] for part in parts_refs])
-        put((t1, t1_low), first, masked(value, first, count))
-
-    blur, blur_back = (k_high, k_low), (kt_high, kt_low)
-    blurred, second, blurred_second = (t1, t1_low), (rf, rf_low), (t2, t2_low)
+        put(blurred, first, masked(value, first, count))
+
 
     def stage(source, weights, target, runs, term=None, sign=1.0):
         terms = [None if term is None else term(keep, kept) for first, count, keep, kept in runs]
-        value = multiply(source, *weights, [run[:2] for run in runs], combine)
+        value = multiply(source, weights, [run[:2] for run in runs], combine)
         start = 0
         for (first, count, keep, kept), added in zip(runs, terms):
             piece = value[start + keep - first : start + keep - first + kept]
@@ -372,7 +376,7 @@
                 piece = added + sign * piece
             put(target, keep, masked(piece, keep, kept))
 
-    receive(x_copies, x_mid, x_from_left, x_from_right, (xf, xf_low), lambda: greet(0), 1, 11)
+    receive(x_copies, x_mid, x_from_left, x_from_right, (xf, xf_low, xf_last), lambda: greet(0), 1, 11)
     take_b()
 
     def remainder(keep, kept):
@@ -382,7 +386,7 @@
     stage(second, blur, blurred_second, [(72, 152, 72, 152)])
     kr0 = own(t2[pl.ds(96, 104), :], 96)
     lr0 = own(smooth(rf, 96, 104), 96)
-    v1 = own(correlate((t2, t2_low), kt_high, kt_low, 96, 104), 96) + lr0
+    v1 = own(correlate(blurred_second, blur_back, 96, 104), 96) + lr0
     spread(v_mid, 4, v1)
     pack_sides(v_mid, v_left, v_right)
     v_copies = field_copies(v_mid, v_left, v_right, v_from_left, v_from_right, v_send, v_recv)
@@ -398,7 +402,7 @@
         meet(1)
         greet(2)
 
-    receive(v_copies, v_mid, v_from_left, v_from_right, (vf, vf_low), meet_and_greet, 2, 10)
+    receive(v_copies, v_mid, v_from_left, v_from_right, (vf, vf_low, vf_last), meet_and_greet, 2, 10)
     smooth_pieces = []
 
     def image(keep, kept):
@@ -454,10 +458,10 @@
     sums = remote(slots.at[others], slots.at[others], sum_send, sum_recv, at(1, 0))
     for copies in (x_copies, b_copies, v_copies):
         sent(copies)
-    stage((vf, vf_low), blur, blurred, [(24, 40, 24, 32), (232, 40, 240, 32)])
+    stage((vf, vf_low, vf_last), blur, blurred, [(24, 40, 24, 32), (232, 40, 240, 32)])
     stage(blurred, blur_back, second, [(48, 40, 48, 32), (208, 40, 216, 32)], image)
     stage(second, blur, blurred_second, [(72, 40, 72, 32), (184, 40, 192, 32)])
-    v3 = own(correlate((t2, t2_low), kt_high, kt_low, 96, 104), 96) + lv2
+    v3 = own(correlate(blurred_second, blur_back, 96, 104), 96) + lv2
     for number, value in enumerate(p + powers(v1, v2, v3)):
         pixels[number] = swap_blocks(value)
     sums.wait_recv()
@@ -533,16 +537,16 @@
         scratch_shapes=[
             middle, middle, b_middle, side, side, side, side, b_side, b_side,
             halo, halo, halo, halo, b_halo, b_halo,
-            flat, flat, flat, flat, flat, flat, flat, flat, flat, flat, flat, flat, flat, flat, flat,
-            pltpu.VMEM((128, 128), F32), pltpu.VMEM((8, 96, 1024), BF16),
-            weight, weight, weight, weight,
+            flat, flat, flat, flat, flat, flat, flat, flat, flat, flat, flat, flat, flat, flat, flat, flat, flat, flat, flat, flat,
+            pltpu.VMEM((128, 128), F32), pltpu.VMEM((8, 144, 1024), BF16),
+            weight, weight, weight, weight, weight, weight,
             tile, tile, tile, tile, tile, tile,
             pltpu.VMEM((n_rows * n_cols, 1, 128), F32), pltpu.VMEM((6, 64, LANES), F32), pltpu.SemaphoreType.REGULAR((3,)), tile, tile, pltpu.VMEM((31, 31), F32), dma((3,)),
             dma((8,)), dma((8,)), dma((8,)), dma((8,)), dma((8,)), dma((8,)),
             dma, dma,
         ],
         compiler_params=pltpu.CompilerParams(
-            collective_id=0, has_side_effects=True, vmem_limit_bytes=16 * 1024 * 1024
+            collective_id=0, has_side_effects=True, vmem_limit_bytes=24 * 1024 * 1024
         ),
     )(*(pltpu.with_memory_space_constraint(x, pltpu.HBM) for x in (right_side, initial_guess, kernel)))
 

time: 29.3 us -> 32.8 us (1.12)
  Pallas kernels: 28.5 us -> 31.9 us
    pallas_call x1, Pallas kernels: 27.8 us -> 31.2 us  [on_device(): pl.pallas_call(body, out_shape=(shape, shape), in_specs=[pl.BlockSpec(mem...]
where the time goes in v10:
time: 32.8 us; the launch traced here: 32.7 us
  Pallas kernels  31.9 us (97%)
  between operations  0.8 us (2%)
    pallas_call x1, Pallas kernels, on_device(): pl.pallas_call(body, out_shape=(shape, shape), in_specs=[pl.BlockSpec(mem...  31.2 us
    pallas_call x1, Pallas kernels, on_device(): pl.pallas_call(store, out_shape=(shape, shape), in_specs=[vmem] * 2, out_...  0.67 us

profile of v10, /device:TPU:1, one launch (start us, length us, event | category | flops | bytes accessed | tf_op | source)
XLA Modules:
  0.0 32.7 jit_solution(7276339995092945637)
XLA Ops:
  0.6 31.2 %shard_map.50 = (f32[64,256]{1,0:T(8,128)S(1)}, f32[64,256]{1,0:T(8,128)S(1)}) custom-call(f32[64,256]{1,0:T(8,128)} %refs_0_.1, f32[64,256]{1,0:T(8,128)} %refs_1_.1, f32[31,31]{1,0:T(8,128)} %refs_2_.1), custom_call_target="tpu_custom_call" | custom-call | tf_op jit(solution)/shard_map/pallas_call | solution.py:532
  31.8 0.7 %shard_map.51 = (f32[64,256]{1,0:T(8,128)}, f32[64,256]{1,0:T(8,128)}) custom-call(f32[64,256]{1,0:T(8,128)S(1)} %get-tuple-element.4.template_ref, f32[64,256]{1,0:T(8,128)S(1)} %get-tuple-element.5.residual_ref), custom_call_target="tpu_custom_call" | custom-call | tf_op jit(solution)/shard_map/pallas_call | solution.py:563

commit v11 on v9

--- a/solution.py
+++ b/solution.py
@@ -167,8 +167,8 @@
         right_ref[pair] = jnp.where(sublane < 4, roll(middle[first, 8:16], 4, 0), middle[second, 8:16])
 
 
-def unpack_middle(middle, flat, masked):
-    for r in range(12):
+def unpack_middle(middle, flat, masked, rows):
+    for r in rows:
         start = PITCH * r + 8
         put(flat, start, masked(middle[r], start, 16))
 
@@ -246,12 +246,12 @@
             dr, dc = DIRECTIONS[number]
             pl.when(exists(-dr, -dc))(copies[number].wait_recv)
 
-    def field_copies(middle, left, right, from_left, from_right, send, recv):
+    def field_copies(middle, left, right, from_left, from_right, send, recv, rows=4):
         copies = []
         for number, (dr, dc) in enumerate(DIRECTIONS):
             if dc == 0:
-                source = middle.at[pl.ds(4, 4)]
-                target = middle.at[pl.ds(4 - 4 * dr, 4)]
+                source = middle.at[pl.ds(4 if dr == -1 else 8 - rows, rows)]
+                target = middle.at[pl.ds(8 if dr == -1 else 4 - rows, rows)]
             else:
                 source = right if dc == 1 else left
                 target = (from_left if dc == 1 else from_right).at[pl.ds(2 - 2 * dr, 2)]
@@ -346,7 +346,7 @@
             return finish
 
         received(copies, range(6, 8))
-        unpack_middle(middle, field, masked)
+        unpack_middle(middle, field, masked, range(top - 1, bottom + 1))
         runs = [(PITCH * r + 8, 16) for r in range(top, bottom)]
         multiply(field, k_high, k_low, runs, keep(runs))
         received(copies, range(6))
@@ -385,8 +385,14 @@
     v1 = own(correlate((t2, t2_low), kt_high, kt_low, 96, 104), 96) + lr0
     spread(v_mid, 4, v1)
     pack_sides(v_mid, v_left, v_right)
-    v_copies = field_copies(v_mid, v_left, v_right, v_from_left, v_from_right, v_send, v_recv)
+    v_copies = field_copies(v_mid, v_left, v_right, v_from_left, v_from_right, v_send, v_recv, 3)
     start(v_copies)
+    far_copies = [
+        remote(v_mid.at[pl.ds(7, 1)], v_mid.at[pl.ds(11, 1)], v_send.at[8], v_recv.at[8], at(-1, 0)),
+        remote(v_mid.at[pl.ds(4, 1)], v_mid.at[pl.ds(0, 1)], v_send.at[9], v_recv.at[9], at(1, 0)),
+    ]
+    pl.when(exists(-1, 0))(far_copies[0].start)
+    pl.when(exists(1, 0))(far_copies[1].start)
     meet(0)
     greet(1)
     r0_own[...] = own(rf[pl.ds(96, 104), :], 96)
@@ -454,6 +460,11 @@
     sums = remote(slots.at[others], slots.at[others], sum_send, sum_recv, at(1, 0))
     for copies in (x_copies, b_copies, v_copies):
         sent(copies)
+    pl.when(exists(-1, 0))(far_copies[0].wait_send)
+    pl.when(exists(1, 0))(far_copies[1].wait_send)
+    pl.when(exists(1, 0))(far_copies[0].wait_recv)
+    pl.when(exists(-1, 0))(far_copies[1].wait_recv)
+    unpack_middle(v_mid, (vf, vf_low), masked, (0, 11))
     stage((vf, vf_low), blur, blurred, [(24, 40, 24, 32), (232, 40, 240, 32)])
     stage(blurred, blur_back, second, [(48, 40, 48, 32), (208, 40, 216, 32)], image)
     stage(second, blur, blurred_second, [(72, 40, 72, 32), (184, 40, 192, 32)])
@@ -538,7 +549,7 @@
             weight, weight, weight, weight,
             tile, tile, tile, tile, tile, tile,
             pltpu.VMEM((n_rows * n_cols, 1, 128), F32), pltpu.VMEM((6, 64, LANES), F32), pltpu.SemaphoreType.REGULAR((3,)), tile, tile, pltpu.VMEM((31, 31), F32), dma((3,)),
-            dma((8,)), dma((8,)), dma((8,)), dma((8,)), dma((8,)), dma((8,)),
+            dma((8,)), dma((8,)), dma((8,)), dma((8,)), dma((10,)), dma((10,)),
             dma, dma,
         ],
         compiler_params=pltpu.CompilerParams(

time: 29.3 us -> 29.3 us (level)
  no operation moved by 1% of the time
where the time goes in v11:
time: 29.3 us; the launch traced here: 29.2 us
  Pallas kernels  28.5 us (97%)
  between operations  0.64 us (2%)
    pallas_call x1, Pallas kernels, on_device(): pl.pallas_call(body, out_shape=(shape, shape), in_specs=[pl.BlockSpec(mem...  27.9 us
    pallas_call x1, Pallas kernels, on_device(): pl.pallas_call(store, out_shape=(shape, shape), in_specs=[vmem] * 2, out_...  0.67 us

profile of v11, /device:TPU:1, one launch (start us, length us, event | category | flops | bytes accessed | tf_op | source)
XLA Modules:
  0.0 29.2 jit_solution(13897563701206791601)
XLA Ops:
  0.6 27.9 %shard_map.50 = (f32[64,256]{1,0:T(8,128)S(1)}, f32[64,256]{1,0:T(8,128)S(1)}) custom-call(f32[64,256]{1,0:T(8,128)} %refs_0_.1, f32[64,256]{1,0:T(8,128)} %refs_1_.1, f32[31,31]{1,0:T(8,128)} %refs_2_.1), custom_call_target="tpu_custom_call" | custom-call | tf_op jit(solution)/shard_map/pallas_call | solution.py:539
  28.5 0.7 %shard_map.51 = (f32[64,256]{1,0:T(8,128)}, f32[64,256]{1,0:T(8,128)}) custom-call(f32[64,256]{1,0:T(8,128)S(1)} %get-tuple-element.4.template_ref, f32[64,256]{1,0:T(8,128)S(1)} %get-tuple-element.5.residual_ref), custom_call_target="tpu_custom_call" | custom-call | tf_op jit(solution)/shard_map/pallas_call | solution.py:570
